TPU v7x, 512 devices: a whole 4x4x16 slice. The times are simulated.
512 devices in a mesh: sector: 32 (over y, x, core), term: 16 (over z).
Axes of the slice: x: 4, y: 4, z: 16, core: 2. Of those that a mesh axis runs over, the one named last changes fastest.
Arguments:
- blocks: bfloat16 [20480, 640], P('sector'), may hold values from -6 to 6
- left_env: bfloat16 [32, 16, 640, 1920], P('sector', 'term'), may hold values from -0.125 to 0.125
- right_env: bfloat16 [32, 16, 640, 640], P('sector', 'term'), may hold values from -0.0625 to 0.0625
- coupling: int32 [32, 3], P('sector'), may hold values 0 or 1
- widths: int32 [32], P('sector'), may hold values from 320 to 640
Outputs:
- filtered: bfloat16 [20480, 640], P('sector')
All inputs are finite; a program needn't handle non-finite values. No bound on the sum of `coupling` on one device may be relied on, other than what follows from the above.
Results may differ from a plain program's by a relative error of at most 0.005.
Values may be sent and summed in bfloat16 or wider, within the bound.
No kernel may reach another device: no remote copies, remote signals or barrier semaphores. Data moves between devices by JAX's collectives and lax.ppermute only.
A program may use at most 64 MiB of HBM per device.

v0:
```python
import jax
import jax.numpy as jnp
from jax import lax
from jax.sharding import PartitionSpec as P


def with_halo(x, sides, width):
    for axis, dim in sides:
        count, length = (lax.axis_size(axis), x.shape[dim])
        up = [(i, (i + 1) % count) for i in range(count - 1)]
        down = [(j, i) for i, j in up]
        last = lax.slice_in_dim(x, length - width, length, axis=dim)
        leading = lax.slice_in_dim(x, 0, width, axis=dim)
        before = lax.ppermute(last, axis, up)
        after = lax.ppermute(leading, axis, down)
        x = jnp.concatenate([before, x, after], axis=dim)
    return x


def keep_live(values, live_width):
    row_index = lax.broadcasted_iota(jnp.int32, values.shape, 0)
    col_index = lax.broadcasted_iota(jnp.int32, values.shape, 1)
    return jnp.where(
        (row_index < live_width) & (col_index < live_width), values, jnp.zeros_like(values)
    )


def contract(stacked, left_part, right_part):
    partial_value = jnp.einsum(
        "tik,kj->tij", left_part, stacked, preferred_element_type=jnp.float32
    ).astype(jnp.bfloat16)
    return jnp.einsum("tij,tjl->il", partial_value, right_part, preferred_element_type=jnp.float32)


def shards(blocks, left_env, right_env, coupling, widths):
    block_side = blocks.shape[1]
    left_part = left_env[0]
    right_part = right_env[0]
    live_width = widths[0]
    row_scale = jnp.repeat(coupling[0].astype(jnp.bfloat16), block_side)

    def full_apply(source):
        nearby = with_halo(source, (("sector", 0),), source.shape[0])
        term_sum = lax.psum(contract(nearby * row_scale[:, None], left_part, right_part), "term")
        return keep_live(term_sum, live_width)

    first_pass = full_apply(blocks).astype(jnp.bfloat16)
    return (2.0 * full_apply(first_pass) - blocks.astype(jnp.float32)).astype(jnp.bfloat16)


def solution(mesh):
    placed = (
        P("sector", None),
        P("sector", "term", None, None),
        P("sector", "term", None, None),
        P("sector", None),
        P("sector"),
    )
    return jax.shard_map(
        shards, mesh=mesh, in_specs=placed, out_specs=P("sector", None), check_vma=False
    )
```

profile of v0, /device:TPU:6, one launch (start us, length us, event | category | flops | bytes accessed | tf_op | source)
XLA Modules:
  0.0 284.3 jit_solution(827276292448857746)
XLA Ops:
  6.5 0.0 copy-start
  6.5 0.0 all-reduce.3.cloned.1.call-start
  6.5 2.3 collective-permute-start.1
  8.8 2.2 collective-permute-start
  11.7 0.7 convert_bitcast_fusion
  12.3 0.1 broadcast_in_dim.3
  12.4 6.6 %collective-permute-done.1 = bf16[640,640]{1,0:T(8,128)(2,1)} collective-permute-done((bf16[640,640]{1,0:T(8,128)(2,1)}, bf16[640,640]{1,0:T(8,128)(2,1)}, u32[]{:S(2)}, u32[]{:S(2)}) %collective-permute-start.1) | collective-permute-done | bytes 819232 | tf_op jit(solution)/shard_map/ppermute | solution.py:15
  19.0 3.8 %collective-permute-done = bf16[640,640]{1,0:T(8,128)(2,1)} collective-permute-done((bf16[640,640]{1,0:T(8,128)(2,1)}, bf16[640,640]{1,0:T(8,128)(2,1)}, u32[]{:S(2)}, u32[]{:S(2)}) %collective-permute-start) | collective-permute-done | bytes 819232 | tf_op jit(solution)/shard_map/ppermute | solution.py:14
  22.8 0.0 copy-done
  22.8 7.2 %fusion.23 = f32[640,640]{1,0:T(8,128)} fusion(bf16[1,1,640,1920]{3,2,1,0:T(8,128)(2,1)S(1)} %copy-done, bf16[640,640]{1,0:T(8,128)(2,1)} %collective-permute-done.1, bf16[640,640]{1,0:T(8,128)(2,1)} %param.5, bf16[640,640]{1,0:T(8,128)(2,1)} %collective-permute-done, bf16[1920]{0:T(1024)(128)(2,1)S(1)} %mul.22, bf16[1,1,640,640]{3,2,1,0:T(8,128)(2,1)} %param.7), kind=kOutput, calls=%fused_computation.22 | convolution fusion | flops 2107392000 | bytes 7376640 | tf_op jit(solution)/shard_map/tij,tjl->il/dot_general | solution.py:32
  30.1 79.9 %all-reduce.4 = bf16[640,640]{1,0:T(8,128)(2,1)S(1)} all-reduce(f32[640,640]{1,0:T(8,128)} %fusion.23), channel_id=1, replica_groups=mesh['sector'=32,'term'=16] {'term'}, use_global_device_ids=true, to_apply=%region_0.0 | all-reduce | flops 409600 | bytes 2457600 | tf_op jit(solution)/shard_map/psum | solution.py:44
  110.0 0.3 fusion.12
  110.3 0.0 copy-start.2
  110.4 0.0 copy-start.1
  110.4 2.1 collective-permute-start.3
  112.4 0.0 copy-done.2
  112.4 2.4 collective-permute-start.2
  114.9 7.4 %collective-permute-done.3 = bf16[640,640]{1,0:T(8,128)(2,1)S(1)} collective-permute-done((bf16[640,640]{1,0:T(8,128)(2,1)S(1)}, bf16[640,640]{1,0:T(8,128)(2,1)S(1)}, u32[]{:S(2)}, u32[]{:S(2)}) %collective-permute-start.3) | collective-permute-done | bytes 819232 | tf_op jit(solution)/shard_map/ppermute | solution.py:15
  122.3 0.0 copy-start.3
  122.3 0.9 copy-done.3
  123.2 3.0 %collective-permute-done.2 = bf16[640,640]{1,0:T(8,128)(2,1)} collective-permute-done((bf16[640,640]{1,0:T(8,128)(2,1)S(1)}, bf16[640,640]{1,0:T(8,128)(2,1)}, u32[]{:S(2)}, u32[]{:S(2)}) %collective-permute-start.2) | collective-permute-done | bytes 819232 | tf_op jit(solution)/shard_map/ppermute | solution.py:14
  126.2 7.2 %fusion.26 = f32[640,640]{1,0:T(8,128)} fusion(bf16[1,1,640,1920]{3,2,1,0:T(8,128)(2,1)S(1)} %copy-done, bf16[640,640]{1,0:T(8,128)(2,1)} %copy-done.3, bf16[640,640]{1,0:T(8,128)(2,1)} %copy-done.2, bf16[640,640]{1,0:T(8,128)(2,1)} %collective-permute-done.2, bf16[1920]{0:T(1024)(128)(2,1)S(1)} %mul.22, bf16[1,1,640,640]{3,2,1,0:T(8,128)(2,1)} %param.7), kind=kOutput, calls=%fused_computation.23 | convolution fusion | flops 2107392000 | bytes 7376640 | tf_op jit(solution)/shard_map/tij,tjl->il/dot_general | solution.py:32
  133.5 0.0 all-reduce.3.cloned.1.call-update
  133.5 141.2 %all-reduce.3.cloned.1.call-done = f32[640,640]{1,0:T(8,128)} async-done(((f32[640,640]{1,0:T(8,128)}), f32[640,640]{1,0:T(8,128)}) %all-reduce.3.cloned.1.call-update) | async-done | bytes 1638416 | tf_op jit(solution)/shard_map/psum | solution.py:44
  274.7 0.0 copy-done.1
  274.7 2.7 fusion.15
  (2 shorter events, 0.0 us)
Async XLA Ops:
  6.5 16.3 %copy-start = (bf16[1,1,640,1920]{3,2,1,0:T(8,128)(2,1)S(1)}, bf16[1,1,640,1920]{3,2,1,0:T(8,128)(2,1)}, u32[]{:S(2)}) copy-start(bf16[1,1,640,1920]{3,2,1,0:T(8,128)(2,1)} %param.6) | copy-start | bytes 7372804
  6.5 268.2 %all-reduce.3.cloned.1.call-start = ((), (), s32[]{:S(2)}) async-start(), calls=%async_computation | async-start | bytes 3276800 | tf_op jit(solution)/shard_map/psum | solution.py:44
  6.5 12.5 %collective-permute-start.1 = (bf16[640,640]{1,0:T(8,128)(2,1)}, bf16[640,640]{1,0:T(8,128)(2,1)}, u32[]{:S(2)}, u32[]{:S(2)}) collective-permute-start(bf16[640,640]{1,0:T(8,128)(2,1)} %param.5), channel_id=1, source_target_pairs={{16,0},{32,16},{48,32},{64,48},{80,64},{96,80},{112,96},{128,112},... | collective-permute-start | bytes 2457608 | tf_op jit(solution)/shard_map/ppermute | solution.py:15
  8.8 14.0 %collective-permute-start = (bf16[640,640]{1,0:T(8,128)(2,1)}, bf16[640,640]{1,0:T(8,128)(2,1)}, u32[]{:S(2)}, u32[]{:S(2)}) collective-permute-start(bf16[640,640]{1,0:T(8,128)(2,1)} %param.5), channel_id=1, source_target_pairs={{0,16},{16,32},{32,48},{48,64},{64,80},{80,96},{96,112},{112,128},... | collective-permute-start | bytes 2457608 | tf_op jit(solution)/shard_map/ppermute | solution.py:14
  110.3 2.1 copy-start.2
  110.4 164.3 %copy-start.1 = (bf16[640,640]{1,0:T(8,128)(2,1)S(1)}, bf16[640,640]{1,0:T(8,128)(2,1)}, u32[]{:S(2)}) copy-start(bf16[640,640]{1,0:T(8,128)(2,1)} %param.5) | copy-start | bytes 2457604
  110.4 11.9 %collective-permute-start.3 = (bf16[640,640]{1,0:T(8,128)(2,1)S(1)}, bf16[640,640]{1,0:T(8,128)(2,1)S(1)}, u32[]{:S(2)}, u32[]{:S(2)}) collective-permute-start(bf16[640,640]{1,0:T(8,128)(2,1)S(1)} %fusion.12), channel_id=1, source_target_pairs={{16,0},{32,16},{48,32},{64,48},{80,64},{96,80},{112,96},{128,112},... | collective-permute-start | bytes 2457608 | tf_op jit(solution)/shard_map/ppermute | solution.py:15
  112.4 13.8 %collective-permute-start.2 = (bf16[640,640]{1,0:T(8,128)(2,1)S(1)}, bf16[640,640]{1,0:T(8,128)(2,1)}, u32[]{:S(2)}, u32[]{:S(2)}) collective-permute-start(bf16[640,640]{1,0:T(8,128)(2,1)S(1)} %fusion.12), channel_id=1, source_target_pairs={{0,16},{16,32},{32,48},{48,64},{64,80},{80,96},{96,112},{112,128},... | collective-permute-start | bytes 2457608 | tf_op jit(solution)/shard_map/ppermute | solution.py:14
  122.3 0.9 copy-start.3
Sparse Core Ops, SparseCore 0:
  133.6 141.0 all-reduce.2
where the time goes:
time: 285 us; the launch traced here: 284 us
  waiting for transfers between devices  162 us (57%)
  blocking collectives  79.9 us (28%)
  matrix products  14.5 us (5%)
  between operations  14.1 us (5%)
  starting transfers between devices  8.91 us (3%)
  other arithmetic  3.72 us (1%)
    psum x1, waiting for transfers between devices, full_apply(): lax.psum(contract(nearby * row_scale[:, None], left_part, right_part), 't...  141 us
    psum x1, blocking collectives, full_apply(): lax.psum(contract(nearby * row_scale[:, None], left_part, right_part), 't...  79.9 us
    dot_general x2, matrix products, contract(): jnp.einsum('tij,tjl->il', partial_value, right_part, preferred_element_ty...  14.5 us
    ppermute x2, waiting for transfers between devices, with_halo(): after = lax.ppermute(leading, axis, down)  14 us
    ppermute x2, waiting for transfers between devices, with_halo(): before = lax.ppermute(last, axis, up)  6.87 us
  transfers between devices with their start and end apart: 5, of which 5 were waited for; matrix products, arithmetic and copies ran while one was open for 0% of the time, Pallas kernels for 0%

commit v1 on v0

v1 whole, which is shorter than its diff:
```python
import jax
import jax.numpy as jnp
from jax import lax
from jax.sharding import PartitionSpec as P


def with_halo(x, axis):
    count = lax.axis_size(axis)
    up = [(i, (i + 1) % count) for i in range(count - 1)]
    down = [(j, i) for i, j in up]
    before = lax.ppermute(x, axis, up)
    after = lax.ppermute(x, axis, down)
    return jnp.concatenate([before, x, after], axis=0)


def keep_live(values, live_width, row_offset):
    row_index = row_offset + lax.broadcasted_iota(jnp.int32, values.shape, 0)
    col_index = lax.broadcasted_iota(jnp.int32, values.shape, 1)
    return jnp.where(
        (row_index < live_width) & (col_index < live_width), values, jnp.zeros_like(values)
    )


def contract(stacked, left_part, right_part):
    partial_value = jnp.einsum(
        "ik,kj->ij", left_part, stacked, preferred_element_type=jnp.float32
    ).astype(jnp.bfloat16)
    return jnp.einsum("ij,jl->il", partial_value, right_part, preferred_element_type=jnp.float32)


def shards(blocks, left_env, right_env, coupling, widths):
    side = blocks.shape[1]
    left_part = left_env[0, 0]
    right_part = right_env[0, 0]
    live_width = widths[0]
    row_scale = jnp.repeat(coupling[0].astype(jnp.bfloat16), side)
    terms = lax.axis_size("term")
    rows = side // terms
    row_offset = lax.axis_index("term") * rows

    def apply_rows(source):
        nearby = with_halo(source, "sector")
        part = contract(nearby * row_scale[:, None], left_part, right_part)
        part = part.astype(jnp.bfloat16).reshape(terms, rows, side)
        pieces = lax.all_to_all(part, "term", 0, 0, tiled=True)
        total = jnp.sum(pieces.astype(jnp.float32), axis=0)
        return keep_live(total, live_width, row_offset)

    def gather(piece):
        return lax.all_gather(piece, "term", axis=0, tiled=True)

    first_pass = gather(apply_rows(blocks).astype(jnp.bfloat16))
    own = lax.dynamic_slice_in_dim(blocks, row_offset, rows, axis=0).astype(jnp.float32)
    return gather((2.0 * apply_rows(first_pass) - own).astype(jnp.bfloat16))


def solution(mesh):
    placed = (
        P("sector", None),
        P("sector", "term", None, None),
        P("sector", "term", None, None),
        P("sector", None),
        P("sector"),
    )
    return jax.shard_map(
        shards, mesh=mesh, in_specs=placed, out_specs=P("sector", None), check_vma=False
    )
```

time: 285 us -> 221 us (0.78)
  waiting for transfers between devices: 162 us -> 99.2 us
  starting transfers between devices: 8.91 us -> 29.1 us
  between operations: 14.1 us -> 0.73 us
  blocking collectives: 79.9 us -> 74 us
    psum x1 -> x0, waiting for transfers between devices: 141 us -> none  [full_apply(): lax.psum(contract(nearby * row_scale[:, None], left_part, right_part), 't...]
    psum x1 -> x0, blocking collectives: 79.9 us -> none  [full_apply(): lax.psum(contract(nearby * row_scale[:, None], left_part, right_part), 't...]
    all_to_all x0 -> x2, waiting for transfers between devices: none -> 77.7 us  [apply_rows(): pieces = lax.all_to_all(part, 'term', 0, 0, tiled=True)]
    all_gather x0 -> x2, blocking collectives: none -> 74 us  [gather(): return lax.all_gather(piece, 'term', axis=0, tiled=True)]
    all_to_all x0 -> x2, starting transfers between devices: none -> 20.4 us  [apply_rows(): pieces = lax.all_to_all(part, 'term', 0, 0, tiled=True)]
  transfers between devices with their start and end apart: 5 -> 6, of which waited for: 5 -> 6; matrix products, arithmetic and copies ran while one was open for 0% -> 0% of each run, Pallas kernels for 0% -> 0%
where the time goes in v1:
time: 221 us; the launch traced here: 220 us
  waiting for transfers between devices  99.2 us (45%)
  blocking collectives  74 us (33%)
  starting transfers between devices  29.1 us (13%)
  matrix products  13.5 us (6%)
    all_to_all x2, waiting for transfers between devices, apply_rows(): pieces = lax.all_to_all(part, 'term', 0, 0, tiled=True)  77.7 us
    all_gather x2, blocking collectives, gather(): return lax.all_gather(piece, 'term', axis=0, tiled=True)  74 us
    all_to_all x2, starting transfers between devices, apply_rows(): pieces = lax.all_to_all(part, 'term', 0, 0, tiled=True)  20.4 us
    ppermute x2, waiting for transfers between devices, with_halo(): after = lax.ppermute(x, axis, down)  14.7 us
    dot_general x2, matrix products, contract(): jnp.einsum('ij,jl->il', partial_value, right_part, preferred_element_type...  13.5 us
    ppermute x2, waiting for transfers between devices, with_halo(): before = lax.ppermute(x, axis, up)  6.86 us
    ppermute x2, starting transfers between devices, with_halo(): before = lax.ppermute(x, axis, up)  4.56 us
  transfers between devices with their start and end apart: 6, of which 6 were waited for; matrix products, arithmetic and copies ran while one was open for 0% of the time, Pallas kernels for 0%

profile of v1, /device:TPU:6, one launch (start us, length us, event | category | flops | bytes accessed | tf_op | source)
XLA Modules:
  0.0 220.3 jit_solution(6024967086172461485)
XLA Ops:
  0.0 0.0 copy-start
  0.0 2.3 %collective-permute-start.1 = (bf16[640,640]{1,0:T(8,128)(2,1)}, bf16[640,640]{1,0:T(8,128)(2,1)S(1)}, u32[]{:S(2)}, u32[]{:S(2)}) collective-permute-start(bf16[640,640]{1,0:T(8,128)(2,1)} %param.5), channel_id=1, source_target_pairs={{16,0},{32,16},{48,32},{64,48},{80,64},{96,80},{112,96},{128,112},... | collective-permute-start | bytes 2457608 | tf_op jit(solution)/shard_map/ppermute | solution.py:12
  2.3 2.2 collective-permute-start
  4.5 0.7 convert_bitcast_fusion
  5.1 0.1 broadcast_in_dim.3
  5.2 7.2 %collective-permute-done.1 = bf16[640,640]{1,0:T(8,128)(2,1)S(1)} collective-permute-done((bf16[640,640]{1,0:T(8,128)(2,1)}, bf16[640,640]{1,0:T(8,128)(2,1)S(1)}, u32[]{:S(2)}, u32[]{:S(2)}) %collective-permute-start.1) | collective-permute-done | bytes 819232 | tf_op jit(solution)/shard_map/ppermute | solution.py:12
  12.5 3.8 %collective-permute-done = bf16[640,640]{1,0:T(8,128)(2,1)} collective-permute-done((bf16[640,640]{1,0:T(8,128)(2,1)}, bf16[640,640]{1,0:T(8,128)(2,1)}, u32[]{:S(2)}, u32[]{:S(2)}) %collective-permute-start) | collective-permute-done | bytes 819232 | tf_op jit(solution)/shard_map/ppermute | solution.py:11
  16.3 0.0 copy-done
  16.3 6.7 %convolution_convert_fusion.1 = bf16[640,640]{1,0:T(8,128)(2,1)} fusion(bf16[1,1,640,1920]{3,2,1,0:T(8,128)(2,1)S(1)} %copy-done, bf16[640,640]{1,0:T(8,128)(2,1)S(1)} %collective-permute-done.1, bf16[640,640]{1,0:T(8,128)(2,1)} %param.5, bf16[640,640]{1,0:T(8,128)(2,1)} %collective-permute-done, bf16[1920]{0:T(1024)(128)(2,1)S(1)} %mul.26, ...), kind=kOutput, calls=%fused_computation.19 | convolution fusion | flops 2107801600 | bytes 6557440 | tf_op jit(solution)/shard_map/ij,jl->il/dot_general | solution.py:28
  23.0 15.2 %all-to-all-start = ((bf16[16,40,640]{2,1,0:T(8,128)(2,1)}), bf16[16,40,640]{2,1,0:T(8,128)(2,1)S(1)}, u32[]{:S(2)}, u32[]{:S(2)}) async-start(bf16[16,40,640]{2,1,0:T(8,128)(2,1)} %bitcast.25), calls=%async_computation | async-start | bytes 1638400 | tf_op jit(solution)/shard_map/all_to_all | solution.py:45
  38.9 40.2 %all-to-all-done = bf16[16,40,640]{2,1,0:T(8,128)(2,1)S(1)} async-done(((bf16[16,40,640]{2,1,0:T(8,128)(2,1)}), bf16[16,40,640]{2,1,0:T(8,128)(2,1)S(1)}, u32[]{:S(2)}, u32[]{:S(2)}) %all-to-all-start) | async-done | bytes 819232 | tf_op jit(solution)/shard_map/all_to_all | solution.py:45
  79.1 0.1 convert_reduce_fusion.1
  79.2 0.1 fusion.26
  79.3 36.7 %all_gather.6 = bf16[640,640]{1,0:T(8,128)(2,1)S(1)} all-gather(bf16[40,640]{1,0:T(8,128)(2,1)S(1)} %fusion.26), channel_id=1, replica_groups=mesh['sector'=32,'term'=16] {'term'}, dimensions={0}, use_global_device_ids=true | all-gather | bytes 870400 | tf_op jit(solution)/shard_map/all_gather | solution.py:50
  116.0 1.9 collective-permute-start.3
  117.9 2.4 %collective-permute-start.2 = (bf16[640,640]{1,0:T(8,128)(2,1)S(1)}, bf16[640,640]{1,0:T(8,128)(2,1)}, u32[]{:S(2)}, u32[]{:S(2)}) collective-permute-start(bf16[640,640]{1,0:T(8,128)(2,1)S(1)} %all_gather.6), channel_id=1, source_target_pairs={{0,16},{16,32},{32,48},{48,64},{64,80},{80,96},{96,112},{112,128},... | collective-permute-start | bytes 2457608 | tf_op jit(solution)/shard_map/ppermute | solution.py:11
  120.3 7.4 %collective-permute-done.3 = bf16[640,640]{1,0:T(8,128)(2,1)S(1)} collective-permute-done((bf16[640,640]{1,0:T(8,128)(2,1)S(1)}, bf16[640,640]{1,0:T(8,128)(2,1)S(1)}, u32[]{:S(2)}, u32[]{:S(2)}) %collective-permute-start.3) | collective-permute-done | bytes 819232 | tf_op jit(solution)/shard_map/ppermute | solution.py:12
  127.7 0.0 copy-start.1
  127.7 0.9 copy-done.1
  128.6 3.0 %collective-permute-done.2 = bf16[640,640]{1,0:T(8,128)(2,1)} collective-permute-done((bf16[640,640]{1,0:T(8,128)(2,1)S(1)}, bf16[640,640]{1,0:T(8,128)(2,1)}, u32[]{:S(2)}, u32[]{:S(2)}) %collective-permute-start.2) | collective-permute-done | bytes 819232 | tf_op jit(solution)/shard_map/ppermute | solution.py:11
  131.7 6.7 %convolution_convert_fusion = bf16[640,640]{1,0:T(8,128)(2,1)} fusion(bf16[1,1,640,1920]{3,2,1,0:T(8,128)(2,1)S(1)} %copy-done, bf16[640,640]{1,0:T(8,128)(2,1)} %copy-done.1, bf16[640,640]{1,0:T(8,128)(2,1)S(1)} %all_gather.6, bf16[640,640]{1,0:T(8,128)(2,1)} %collective-permute-done.2, bf16[1920]{0:T(1024)(128)(2,1)S(1)} %mul.26, ...), kind=kOutput, calls=%fused_computation.18 | convolution fusion | flops 2107801600 | bytes 6557440 | tf_op jit(solution)/shard_map/ij,jl->il/dot_general | solution.py:28
  138.4 5.2 %all-to-all-start.1 = ((bf16[16,40,640]{2,1,0:T(8,128)(2,1)}), bf16[16,40,640]{2,1,0:T(8,128)(2,1)S(1)}, u32[]{:S(2)}, u32[]{:S(2)}) async-start(bf16[16,40,640]{2,1,0:T(8,128)(2,1)} %bitcast.26), calls=%async_computation.1 | async-start | bytes 1638400 | tf_op jit(solution)/shard_map/all_to_all | solution.py:45
  143.6 37.5 %all-to-all-done.1 = bf16[16,40,640]{2,1,0:T(8,128)(2,1)S(1)} async-done(((bf16[16,40,640]{2,1,0:T(8,128)(2,1)}), bf16[16,40,640]{2,1,0:T(8,128)(2,1)S(1)}, u32[]{:S(2)}, u32[]{:S(2)}) %all-to-all-start.1) | async-done | bytes 819232 | tf_op jit(solution)/shard_map/all_to_all | solution.py:45
  181.1 0.1 convert_reduce_fusion
  181.2 0.9 fusion.29
  182.2 37.2 %all_gather.7 = bf16[640,640]{1,0:T(8,128)(2,1)S(1)} all-gather(bf16[40,640]{1,0:T(8,128)(2,1)S(1)} %fusion.29), channel_id=1, replica_groups=mesh['sector'=32,'term'=16] {'term'}, dimensions={0}, use_global_device_ids=true | all-gather | bytes 870400 | tf_op jit(solution)/shard_map/all_gather | solution.py:50
  219.4 0.9 copy.8
  (3 shorter events, 0.0 us)
Async XLA Ops:
  0.0 16.3 %copy-start = (bf16[1,1,640,1920]{3,2,1,0:T(8,128)(2,1)S(1)}, bf16[1,1,640,1920]{3,2,1,0:T(8,128)(2,1)}, u32[]{:S(2)}) copy-start(bf16[1,1,640,1920]{3,2,1,0:T(8,128)(2,1)} %param.6) | copy-start | bytes 7372804
  0.0 12.5 %collective-permute-start.1 = (bf16[640,640]{1,0:T(8,128)(2,1)}, bf16[640,640]{1,0:T(8,128)(2,1)S(1)}, u32[]{:S(2)}, u32[]{:S(2)}) collective-permute-start(bf16[640,640]{1,0:T(8,128)(2,1)} %param.5), channel_id=1, source_target_pairs={{16,0},{32,16},{48,32},{64,48},{80,64},{96,80},{112,96},{128,112},... | collective-permute-start | bytes 2457608 | tf_op jit(solution)/shard_map/ppermute | solution.py:12
  2.3 14.0 %collective-permute-start = (bf16[640,640]{1,0:T(8,128)(2,1)}, bf16[640,640]{1,0:T(8,128)(2,1)}, u32[]{:S(2)}, u32[]{:S(2)}) collective-permute-start(bf16[640,640]{1,0:T(8,128)(2,1)} %param.5), channel_id=1, source_target_pairs={{0,16},{16,32},{32,48},{48,64},{64,80},{80,96},{96,112},{112,128},... | collective-permute-start | bytes 2457608 | tf_op jit(solution)/shard_map/ppermute | solution.py:11
  23.0 56.0 %all-to-all-start = ((bf16[16,40,640]{2,1,0:T(8,128)(2,1)}), bf16[16,40,640]{2,1,0:T(8,128)(2,1)S(1)}, u32[]{:S(2)}, u32[]{:S(2)}) async-start(bf16[16,40,640]{2,1,0:T(8,128)(2,1)} %bitcast.25), calls=%async_computation | async-start | bytes 1638400 | tf_op jit(solution)/shard_map/all_to_all | solution.py:45
  116.0 11.8 %collective-permute-start.3 = (bf16[640,640]{1,0:T(8,128)(2,1)S(1)}, bf16[640,640]{1,0:T(8,128)(2,1)S(1)}, u32[]{:S(2)}, u32[]{:S(2)}) collective-permute-start(bf16[640,640]{1,0:T(8,128)(2,1)S(1)} %all_gather.6), channel_id=1, source_target_pairs={{16,0},{32,16},{48,32},{64,48},{80,64},{96,80},{112,96},{128,112},... | collective-permute-start | bytes 2457608 | tf_op jit(solution)/shard_map/ppermute | solution.py:12
  117.9 13.8 %collective-permute-start.2 = (bf16[640,640]{1,0:T(8,128)(2,1)S(1)}, bf16[640,640]{1,0:T(8,128)(2,1)}, u32[]{:S(2)}, u32[]{:S(2)}) collective-permute-start(bf16[640,640]{1,0:T(8,128)(2,1)S(1)} %all_gather.6), channel_id=1, source_target_pairs={{0,16},{16,32},{32,48},{48,64},{64,80},{80,96},{96,112},{112,128},... | collective-permute-start | bytes 2457608 | tf_op jit(solution)/shard_map/ppermute | solution.py:11
  127.7 0.9 copy-start.1
  138.4 42.7 %all-to-all-start.1 = ((bf16[16,40,640]{2,1,0:T(8,128)(2,1)}), bf16[16,40,640]{2,1,0:T(8,128)(2,1)S(1)}, u32[]{:S(2)}, u32[]{:S(2)}) async-start(bf16[16,40,640]{2,1,0:T(8,128)(2,1)} %bitcast.26), calls=%async_computation.1 | async-start | bytes 1638400 | tf_op jit(solution)/shard_map/all_to_all | solution.py:45

commit v2 on v1

--- a/solution.py
+++ b/solution.py
@@ -34,24 +34,15 @@
     right_part = right_env[0, 0]
     live_width = widths[0]
     row_scale = jnp.repeat(coupling[0].astype(jnp.bfloat16), side)
-    terms = lax.axis_size("term")
-    rows = side // terms
-    row_offset = lax.axis_index("term") * rows
 
-    def apply_rows(source):
+    def live_part(source):
         nearby = with_halo(source, "sector")
-        part = contract(nearby * row_scale[:, None], left_part, right_part)
-        part = part.astype(jnp.bfloat16).reshape(terms, rows, side)
-        pieces = lax.all_to_all(part, "term", 0, 0, tiled=True)
-        total = jnp.sum(pieces.astype(jnp.float32), axis=0)
-        return keep_live(total, live_width, row_offset)
+        return keep_live(contract(nearby * row_scale[:, None], left_part, right_part), live_width, 0)
 
-    def gather(piece):
-        return lax.all_gather(piece, "term", axis=0, tiled=True)
-
-    first_pass = gather(apply_rows(blocks).astype(jnp.bfloat16))
-    own = lax.dynamic_slice_in_dim(blocks, row_offset, rows, axis=0).astype(jnp.float32)
-    return gather((2.0 * apply_rows(first_pass) - own).astype(jnp.bfloat16))
+    first_pass = lax.psum(live_part(blocks), "term").astype(jnp.bfloat16)
+    once = jnp.where(lax.axis_index("term") == 0, 1.0, 0.0)
+    second = 2.0 * live_part(first_pass) - once * blocks.astype(jnp.float32)
+    return lax.psum(second, "term").astype(jnp.bfloat16)
 
 
 def solution(mesh):

time: 221 us -> 201 us (0.910); the launches traced: 220 us -> 198 us
  waiting for transfers between devices: 99.2 us -> 21.8 us
  blocking collectives: 74 us -> 151 us
  starting transfers between devices: 29.1 us -> 8.78 us
    psum x0 -> x2, blocking collectives: none -> 151 us  [the longest x1 79.9 us: shards(): first_pass = lax.psum(live_part(blocks), 'term').astype(jnp.bfloat16)]
    all_to_all x2 -> x0, waiting for transfers between devices: 77.7 us -> none  [apply_rows(): pieces = lax.all_to_all(part, 'term', 0, 0, tiled=True)]
    all_gather x2 -> x0, blocking collectives: 74 us -> none  [gather(): return lax.all_gather(piece, 'term', axis=0, tiled=True)]
    all_to_all x2 -> x0, starting transfers between devices: 20.4 us -> none  [apply_rows(): pieces = lax.all_to_all(part, 'term', 0, 0, tiled=True)]
  transfers between devices with their start and end apart: 6 -> 4, of which waited for: 6 -> 4; matrix products, arithmetic and copies ran while one was open for 0% -> 0% of each run, Pallas kernels for 0% -> 0%
where the time goes in v2:
time: 201 us; the launch traced here: 198 us
  blocking collectives  151 us (75%)
  waiting for transfers between devices  21.8 us (11%)
  matrix products  14.3 us (7%)
  starting transfers between devices  8.78 us (4%)
    psum x1, blocking collectives, shards(): first_pass = lax.psum(live_part(blocks), 'term').astype(jnp.bfloat16)  79.9 us
    psum x1, blocking collectives, shards(): return lax.psum(second, 'term').astype(jnp.bfloat16)  71.5 us
    dot_general x2, matrix products, contract(): jnp.einsum('ij,jl->il', partial_value, right_part, preferred_element_type...  14.3 us
    ppermute x2, waiting for transfers between devices, with_halo(): after = lax.ppermute(x, axis, down)  14 us
    ppermute x2, waiting for transfers between devices, with_halo(): before = lax.ppermute(x, axis, up)  7.75 us
    ppermute x2, starting transfers between devices, with_halo(): before = lax.ppermute(x, axis, up)  4.56 us
    ppermute x2, starting transfers between devices, with_halo(): after = lax.ppermute(x, axis, down)  4.22 us
  transfers between devices with their start and end apart: 4, of which 4 were waited for; matrix products, arithmetic and copies ran while one was open for 0% of the time, Pallas kernels for 0%

profile of v2, /device:TPU:6, one launch (start us, length us, event | category | flops | bytes accessed | tf_op | source)
XLA Modules:
  0.0 197.7 jit_solution(907089884934032647)
XLA Ops:
  0.0 0.0 copy-start
  0.0 2.3 %collective-permute-start.1 = (bf16[640,640]{1,0:T(8,128)(2,1)}, bf16[640,640]{1,0:T(8,128)(2,1)S(1)}, u32[]{:S(2)}, u32[]{:S(2)}) collective-permute-start(bf16[640,640]{1,0:T(8,128)(2,1)} %param.5), channel_id=1, source_target_pairs={{16,0},{32,16},{48,32},{64,48},{80,64},{96,80},{112,96},{128,112},... | collective-permute-start | bytes 2457608 | tf_op jit(solution)/shard_map/ppermute | solution.py:12
  2.3 2.2 %collective-permute-start = (bf16[640,640]{1,0:T(8,128)(2,1)}, bf16[640,640]{1,0:T(8,128)(2,1)}, u32[]{:S(2)}, u32[]{:S(2)}) collective-permute-start(bf16[640,640]{1,0:T(8,128)(2,1)} %param.5), channel_id=1, source_target_pairs={{0,16},{16,32},{32,48},{48,64},{64,80},{80,96},{96,112},{112,128},... | collective-permute-start | bytes 2457608 | tf_op jit(solution)/shard_map/ppermute | solution.py:11
  5.1 0.7 convert_bitcast_fusion
  5.8 0.1 broadcast_in_dim.3
  5.9 6.6 %collective-permute-done.1 = bf16[640,640]{1,0:T(8,128)(2,1)S(1)} collective-permute-done((bf16[640,640]{1,0:T(8,128)(2,1)}, bf16[640,640]{1,0:T(8,128)(2,1)S(1)}, u32[]{:S(2)}, u32[]{:S(2)}) %collective-permute-start.1) | collective-permute-done | bytes 819232 | tf_op jit(solution)/shard_map/ppermute | solution.py:12
  12.5 3.8 %collective-permute-done = bf16[640,640]{1,0:T(8,128)(2,1)} collective-permute-done((bf16[640,640]{1,0:T(8,128)(2,1)}, bf16[640,640]{1,0:T(8,128)(2,1)}, u32[]{:S(2)}, u32[]{:S(2)}) %collective-permute-start) | collective-permute-done | bytes 819232 | tf_op jit(solution)/shard_map/ppermute | solution.py:11
  16.3 0.0 copy-done
  16.3 7.0 %and_select_fusion.1 = f32[640,640]{1,0:T(8,128)} fusion(bf16[1,1,640,1920]{3,2,1,0:T(8,128)(2,1)S(1)} %copy-done, bf16[640,640]{1,0:T(8,128)(2,1)S(1)} %collective-permute-done.1, bf16[640,640]{1,0:T(8,128)(2,1)} %param.5, bf16[640,640]{1,0:T(8,128)(2,1)} %collective-permute-done, bf16[1920]{0:T(1024)(128)(2,1)S(1)} %mul.28, ...), kind=kOutput, calls=%fused_computation.15 | convolution fusion | flops 2108211200 | bytes 7377280 | tf_op jit(solution)/shard_map/ij,jl->il/dot_general | solution.py:28
  23.3 79.9 %all-reduce.2 = bf16[640,640]{1,0:T(8,128)(2,1)S(1)} all-reduce(f32[640,640]{1,0:T(8,128)} %and_select_fusion.1), channel_id=1, replica_groups=mesh['sector'=32,'term'=16] {'term'}, use_global_device_ids=true, to_apply=%region_0.1 | all-reduce | flops 409600 | bytes 2457600 | tf_op jit(solution)/shard_map/psum | solution.py:42
  103.2 1.9 collective-permute-start.3
  105.2 2.4 %collective-permute-start.2 = (bf16[640,640]{1,0:T(8,128)(2,1)S(1)}, bf16[640,640]{1,0:T(8,128)(2,1)}, u32[]{:S(2)}, u32[]{:S(2)}) collective-permute-start(bf16[640,640]{1,0:T(8,128)(2,1)S(1)} %all-reduce.2), channel_id=1, source_target_pairs={{0,16},{16,32},{32,48},{48,64},{64,80},{80,96},{96,112},{112,128},... | collective-permute-start | bytes 2457608 | tf_op jit(solution)/shard_map/ppermute | solution.py:11
  107.6 7.4 %collective-permute-done.3 = bf16[640,640]{1,0:T(8,128)(2,1)} collective-permute-done((bf16[640,640]{1,0:T(8,128)(2,1)S(1)}, bf16[640,640]{1,0:T(8,128)(2,1)}, u32[]{:S(2)}, u32[]{:S(2)}) %collective-permute-start.3) | collective-permute-done | bytes 819232 | tf_op jit(solution)/shard_map/ppermute | solution.py:12
  115.0 3.9 %collective-permute-done.2 = bf16[640,640]{1,0:T(8,128)(2,1)} collective-permute-done((bf16[640,640]{1,0:T(8,128)(2,1)S(1)}, bf16[640,640]{1,0:T(8,128)(2,1)}, u32[]{:S(2)}, u32[]{:S(2)}) %collective-permute-start.2) | collective-permute-done | bytes 819232 | tf_op jit(solution)/shard_map/ppermute | solution.py:11
  118.9 7.3 %fusion.13 = f32[640,640]{1,0:T(8,128)} fusion(bf16[640,640]{1,0:T(8,128)(2,1)} %param.5, bf16[1,1,640,640]{3,2,1,0:T(8,128)(2,1)} %param.7, f32[]{:T(128)S(6)} %select_n.13, pred[640]{0:T(1024)(128)(4,1)S(1)} %iota_compare_fusion, bf16[1,1,640,1920]{3,2,1,0:T(8,128)(2,1)S(1)} %copy-done, bf16[640,640]{1,0:T(8,128)(2,1)} %collective-permute-done.3, ...), kind=kOutput, calls=%fused_computation.17 | convolution fusion | flops 2109849600 | bytes 8196484 | tf_op jit(solution)/shard_map/ij,jl->il/dot_general | solution.py:28
  126.2 71.5 %all-reduce.3 = bf16[640,640]{1,0:T(8,128)(2,1)} all-reduce(f32[640,640]{1,0:T(8,128)} %fusion.13), channel_id=1, replica_groups=mesh['sector'=32,'term'=16] {'term'}, use_global_device_ids=true, to_apply=%region_1.2 | all-reduce | flops 409600 | bytes 2457600 | tf_op jit(solution)/shard_map/psum | solution.py:45
  (2 shorter events, 0.0 us)
Async XLA Ops:
  0.0 16.3 %copy-start = (bf16[1,1,640,1920]{3,2,1,0:T(8,128)(2,1)S(1)}, bf16[1,1,640,1920]{3,2,1,0:T(8,128)(2,1)}, u32[]{:S(2)}) copy-start(bf16[1,1,640,1920]{3,2,1,0:T(8,128)(2,1)} %param.6) | copy-start | bytes 7372804
  0.0 12.5 %collective-permute-start.1 = (bf16[640,640]{1,0:T(8,128)(2,1)}, bf16[640,640]{1,0:T(8,128)(2,1)S(1)}, u32[]{:S(2)}, u32[]{:S(2)}) collective-permute-start(bf16[640,640]{1,0:T(8,128)(2,1)} %param.5), channel_id=1, source_target_pairs={{16,0},{32,16},{48,32},{64,48},{80,64},{96,80},{112,96},{128,112},... | collective-permute-start | bytes 2457608 | tf_op jit(solution)/shard_map/ppermute | solution.py:12
  2.3 14.0 %collective-permute-start = (bf16[640,640]{1,0:T(8,128)(2,1)}, bf16[640,640]{1,0:T(8,128)(2,1)}, u32[]{:S(2)}, u32[]{:S(2)}) collective-permute-start(bf16[640,640]{1,0:T(8,128)(2,1)} %param.5), channel_id=1, source_target_pairs={{0,16},{16,32},{32,48},{48,64},{64,80},{80,96},{96,112},{112,128},... | collective-permute-start | bytes 2457608 | tf_op jit(solution)/shard_map/ppermute | solution.py:11
  103.2 11.8 %collective-permute-start.3 = (bf16[640,640]{1,0:T(8,128)(2,1)S(1)}, bf16[640,640]{1,0:T(8,128)(2,1)}, u32[]{:S(2)}, u32[]{:S(2)}) collective-permute-start(bf16[640,640]{1,0:T(8,128)(2,1)S(1)} %all-reduce.2), channel_id=1, source_target_pairs={{16,0},{32,16},{48,32},{64,48},{80,64},{96,80},{112,96},{128,112},... | collective-permute-start | bytes 2457608 | tf_op jit(solution)/shard_map/ppermute | solution.py:12
  105.2 13.8 %collective-permute-start.2 = (bf16[640,640]{1,0:T(8,128)(2,1)S(1)}, bf16[640,640]{1,0:T(8,128)(2,1)}, u32[]{:S(2)}, u32[]{:S(2)}) collective-permute-start(bf16[640,640]{1,0:T(8,128)(2,1)S(1)} %all-reduce.2), channel_id=1, source_target_pairs={{0,16},{16,32},{32,48},{48,64},{64,80},{80,96},{96,112},{112,128},... | collective-permute-start | bytes 2457608 | tf_op jit(solution)/shard_map/ppermute | solution.py:11

commit v3 on v2

v3 whole, which is shorter than its diff:
```python
import functools

import jax
import jax.numpy as jnp
from jax import lax
from jax.experimental import pallas as pl
from jax.experimental.pallas import tpu as pltpu
from jax.sharding import PartitionSpec as P


ROW_STEPS = 2


def early_body(where, coupled, left_own, own, left_mate, mate, total):
    mate_at = where[0]
    own_part = jnp.dot(left_own[...], own[...], preferred_element_type=jnp.float32)
    mate_part = jnp.dot(left_mate[...], mate[...], preferred_element_type=jnp.float32)
    total[...] = (
        coupled[1].astype(jnp.float32) * own_part
        + coupled[mate_at].astype(jnp.float32) * mate_part
    )


def late_body(where, coupled, width, early, left_far, far, right, *rest, second):
    far_at = 2 - where[0]
    live_width = width[0]
    out = rest[-1]
    far_part = jnp.dot(left_far[...], far[...], preferred_element_type=jnp.float32)
    partial = (early[...] + coupled[far_at].astype(jnp.float32) * far_part).astype(jnp.bfloat16)
    summed = jnp.dot(partial, right[...], preferred_element_type=jnp.float32)
    rows = summed.shape[0]
    row_index = pl.program_id(0) * rows + lax.broadcasted_iota(jnp.int32, summed.shape, 0)
    col_index = lax.broadcasted_iota(jnp.int32, summed.shape, 1)
    live = (row_index < live_width) & (col_index < live_width)
    summed = jnp.where(live, summed, jnp.zeros_like(summed))
    if second:
        once = where[1].astype(jnp.float32)
        summed = 2.0 * summed - once * rest[0][...].astype(jnp.float32)
    out[...] = summed


def early_product(where, coupled, left_part, own, mate):
    side = own.shape[1]
    whole = lambda i, where, coupled: (0, 0)
    return pl.pallas_call(
        early_body,
        grid_spec=pltpu.PrefetchScalarGridSpec(
            num_scalar_prefetch=2,
            grid=(1,),
            in_specs=[
                pl.BlockSpec((side, side), lambda i, where, coupled: (0, 1)),
                pl.BlockSpec((side, side), whole),
                pl.BlockSpec((side, side), lambda i, where, coupled: (0, where[0])),
                pl.BlockSpec((side, side), whole),
            ],
            out_specs=pl.BlockSpec((side, side), whole),
        ),
        out_shape=jax.ShapeDtypeStruct((side, side), jnp.float32),
        cost_estimate=pl.CostEstimate(
            flops=4 * side**3, bytes_accessed=12 * side * side, transcendentals=0
        ),
        name="early_product",
    )(where, coupled, left_part, own, left_part, mate)


def late_product(where, coupled, width, early, left_part, far, right_part, base=None):
    side = far.shape[1]
    rows = side // ROW_STEPS
    whole = lambda i, *_: (0, 0)
    by_rows = pl.BlockSpec((rows, side), lambda i, *_: (i, 0))
    in_specs = [
        by_rows,
        pl.BlockSpec((rows, side), lambda i, where, *_: (i, 2 - where[0])),
        pl.BlockSpec((side, side), whole),
        pl.BlockSpec((side, side), whole),
    ]
    operands = [early, left_part, far, right_part]
    if base is not None:
        in_specs.append(by_rows)
        operands.append(base)
    return pl.pallas_call(
        functools.partial(late_body, second=base is not None),
        grid_spec=pltpu.PrefetchScalarGridSpec(
            num_scalar_prefetch=3, grid=(ROW_STEPS,), in_specs=in_specs, out_specs=by_rows
        ),
        out_shape=jax.ShapeDtypeStruct((side, side), jnp.float32),
        cost_estimate=pl.CostEstimate(
            flops=4 * side**3, bytes_accessed=16 * side * side, transcendentals=0
        ),
        name="late_product",
    )(where, coupled, width, *operands)


def shards(blocks, left_env, right_env, coupling, widths):
    left_part = left_env[0, 0]
    right_part = right_env[0, 0]
    coupled = coupling[0]
    count = lax.axis_size("sector")
    sector = lax.axis_index("sector")
    mate_at = jnp.where(sector % 2 == 0, 2, 0).astype(jnp.int32)
    once = (lax.axis_index("term") == 0).astype(jnp.int32)
    where = jnp.stack([mate_at, once])
    across = [(i, i + 1) for i in range(1, count - 1, 2)]
    across += [(j, i) for i, j in across]
    within = [(i, i ^ 1) for i in range(count)]

    def live_part(source, base=None):
        far = lax.ppermute(source, "sector", across)
        mate = lax.ppermute(source, "sector", within)
        early = early_product(where, coupled, left_part, source, mate)
        return late_product(where, coupled, widths, early, left_part, far, right_part, base)

    first_pass = lax.psum(live_part(blocks), "term").astype(jnp.bfloat16)
    return lax.psum(live_part(first_pass, blocks), "term").astype(jnp.bfloat16)


def solution(mesh):
    placed = (
        P("sector", None),
        P("sector", "term", None, None),
        P("sector", "term", None, None),
        P("sector", None),
        P("sector"),
    )
    return jax.shard_map(
        shards, mesh=mesh, in_specs=placed, out_specs=P("sector", None), check_vma=False
    )
```

time: 201 us -> 198 us (0.985)
  the two profiles are of different devices: /device:TPU:6 before, /device:TPU:24 now
where the time goes in v3:
time: 198 us
  blocking collectives  150 us (76%)
  Pallas kernels  21.3 us (11%)
  starting transfers between devices  12.2 us (6%)
  waiting for transfers between devices  9.61 us (5%)
  local copies, waits for them, and re-layouts  3.56 us (2%)
    psum x1, blocking collectives, shards(): first_pass = lax.psum(live_part(blocks), 'term').astype(jnp.bfloat16)  78.5 us
    psum x1, blocking collectives, shards(): return lax.psum(live_part(first_pass, blocks), 'term').astype(jnp.bfloat16)  71.5 us
    pallas_call x2, Pallas kernels, early_product(): pl.pallas_call(early_body, grid_spec=pltpu.PrefetchScalarGridSpec(num_sca...  10.7 us
    pallas_call x2, Pallas kernels, late_product(): pl.pallas_call(functools.partial(late_body, second=base is not None), gri...  10.6 us
    ppermute x2, waiting for transfers between devices, live_part(): far = lax.ppermute(source, 'sector', across)  9.6 us
    ppermute x2, starting transfers between devices, live_part(): far = lax.ppermute(source, 'sector', across)  8.33 us
  transfers between devices with their start and end apart: 4, of which 2 were waited for; matrix products, arithmetic and copies ran while one was open for 0% of the time, Pallas kernels for 5%

profile of v3, /device:TPU:24, one launch (start us, length us, event | category | flops | bytes accessed | tf_op | source)
XLA Modules:
  0.0 198.0 jit_solution(9449573502801837043)
XLA Ops:
  0.0 1.9 collective-permute-start
  1.9 5.0 %collective-permute-start.1 = (bf16[640,640]{1,0:T(8,128)(2,1)}, bf16[640,640]{1,0:T(8,128)(2,1)S(1)}, u32[]{:S(2)}, u32[]{:S(2)}) collective-permute-start(bf16[640,640]{1,0:T(8,128)(2,1)} %rest_0_.1), channel_id=1, source_target_pairs={{16,32},{48,64},{80,96},{112,128},{144,160},{176,192},{208,224},{2... | collective-permute-start | bytes 2457608 | tf_op jit(solution)/shard_map/ppermute | solution.py:108
  7.5 0.6 pad_add_fusion.where
  8.2 0.0 collective-permute-done.mate
  8.2 0.0 copy-start.1
  8.2 0.9 copy-done.1
  9.1 5.3 %early_product.2.early = f32[640,640]{1,0:T(8,128)} custom-call(s32[2]{0:T(128)} %pad_add_fusion.where, s32[3]{0:T(128)} %bitcast.13, bf16[640,1920]{1,0:T(8,128)(2,1)} %bitcast.5, bf16[640,640]{1,0:T(8,128)(2,1)} %rest_0_.1, bf16[640,1920]{1,0:T(8,128)(2,1)} %bitcast.6, bf16[640,640]{1,0:T(8,128)(2,1)} %copy-done.1), custom_call_target="tpu_custom_call" | custom-call | flops 1048576000 | bytes 4915200 | tf_op jit(solution)/shard_map/early_product/pallas_call | solution.py:45
  14.4 3.5 %collective-permute-done.1.far = bf16[640,640]{1,0:T(8,128)(2,1)S(1)} collective-permute-done((bf16[640,640]{1,0:T(8,128)(2,1)}, bf16[640,640]{1,0:T(8,128)(2,1)S(1)}, u32[]{:S(2)}, u32[]{:S(2)}) %collective-permute-start.1) | collective-permute-done | bytes 819232 | tf_op jit(solution)/shard_map/ppermute | solution.py:108
  17.9 0.0 copy-start.4
  17.9 0.9 copy-done.4
  18.8 5.2 %late_product.2 = f32[640,640]{1,0:T(8,128)} custom-call(s32[2]{0:T(128)} %pad_add_fusion.where, s32[3]{0:T(128)} %bitcast.14, s32[1]{0:T(128)S(6)} %copy.10.width, f32[640,640]{1,0:T(8,128)} %early_product.2.early, bf16[640,1920]{1,0:T(8,128)(2,1)} %bitcast.7, bf16[640,640]{1,0:T(8,128)(2,1)} %copy-done.4, bf16[640,640]{1,0:T(8,128)(2,1)} %bitcast.11), custom_call_target="tpu_custom_call" | custom-call | flops 1048576000 | bytes 6553600 | tf_op jit(solution)/shard_map/late_product/pallas_call | solution.py:81
  24.0 78.5 %all-reduce.2.own = bf16[640,640]{1,0:T(8,128)(2,1)S(1)} all-reduce(f32[640,640]{1,0:T(8,128)} %late_product.2), channel_id=1, replica_groups=mesh['sector'=32,'term'=16] {'term'}, use_global_device_ids=true, to_apply=%region_0.1 | all-reduce | flops 409600 | bytes 2457600 | tf_op jit(solution)/shard_map/psum | solution.py:113
  102.4 0.0 copy-start
  102.4 1.9 collective-permute-start.2
  104.4 3.4 %collective-permute-start.3 = (bf16[640,640]{1,0:T(8,128)(2,1)S(1)}, bf16[640,640]{1,0:T(8,128)(2,1)S(1)}, u32[]{:S(2)}, u32[]{:S(2)}) collective-permute-start(bf16[640,640]{1,0:T(8,128)(2,1)S(1)} %all-reduce.2.own), channel_id=1, source_target_pairs={{16,32},{48,64},{80,96},{112,128},{144,160},{176,192},{208,224},{2... | collective-permute-start | bytes 2457608 | tf_op jit(solution)/shard_map/ppermute | solution.py:108
  107.8 0.0 collective-permute-done.2.mate
  107.8 0.0 copy-done
  107.8 0.0 copy-start.3
  107.8 0.9 copy-done.3
  108.7 5.3 %early_product.3.early = f32[640,640]{1,0:T(8,128)} custom-call(s32[2]{0:T(128)} %pad_add_fusion.where, s32[3]{0:T(128)} %bitcast.15, bf16[640,1920]{1,0:T(8,128)(2,1)} %bitcast.8, bf16[640,640]{1,0:T(8,128)(2,1)} %copy-done, bf16[640,1920]{1,0:T(8,128)(2,1)} %bitcast.9, bf16[640,640]{1,0:T(8,128)(2,1)} %copy-done.3), custom_call_target="tpu_custom_call" | custom-call | flops 1048576000 | bytes 4915200 | tf_op jit(solution)/shard_map/early_product/pallas_call | solution.py:45
  114.0 6.1 %collective-permute-done.3.far = bf16[640,640]{1,0:T(8,128)(2,1)S(1)} collective-permute-done((bf16[640,640]{1,0:T(8,128)(2,1)S(1)}, bf16[640,640]{1,0:T(8,128)(2,1)S(1)}, u32[]{:S(2)}, u32[]{:S(2)}) %collective-permute-start.3) | collective-permute-done | bytes 819232 | tf_op jit(solution)/shard_map/ppermute | solution.py:108
  120.1 0.0 copy-start.2
  120.1 0.9 copy-done.2
  121.0 5.4 %late_product.3 = f32[640,640]{1,0:T(8,128)} custom-call(s32[2]{0:T(128)} %pad_add_fusion.where, s32[3]{0:T(128)} %bitcast.16, s32[1]{0:T(128)S(6)} %copy.10.width, f32[640,640]{1,0:T(8,128)} %early_product.3.early, bf16[640,1920]{1,0:T(8,128)(2,1)} %bitcast.10, bf16[640,640]{1,0:T(8,128)(2,1)} %copy-done.2, bf16[640,640]{1,0:T(8,128)(2,1)} %bitcast.12, ...), custom_call_target="tpu_custom_call" | custom-call | flops 1048576000 | bytes 6553600 | tf_op jit(solution)/shard_map/late_product/pallas_call | solution.py:81
  126.5 71.5 %all-reduce.3 = bf16[640,640]{1,0:T(8,128)(2,1)} all-reduce(f32[640,640]{1,0:T(8,128)} %late_product.3), channel_id=1, replica_groups=mesh['sector'=32,'term'=16] {'term'}, use_global_device_ids=true, to_apply=%region_1.2 | all-reduce | flops 409600 | bytes 2457600 | tf_op jit(solution)/shard_map/psum | solution.py:114
Async XLA Ops:
  0.0 8.2 %collective-permute-start = (bf16[640,640]{1,0:T(8,128)(2,1)}, bf16[640,640]{1,0:T(8,128)(2,1)S(1)}, u32[]{:S(2)}, u32[]{:S(2)}) collective-permute-start(bf16[640,640]{1,0:T(8,128)(2,1)} %rest_0_.1), channel_id=1, source_target_pairs={{0,16},{16,0},{32,48},{48,32},{64,80},{80,64},{96,112},{112,96},{1... | collective-permute-start | bytes 2457608 | tf_op jit(solution)/shard_map/ppermute | solution.py:109
  1.9 16.0 %collective-permute-start.1 = (bf16[640,640]{1,0:T(8,128)(2,1)}, bf16[640,640]{1,0:T(8,128)(2,1)S(1)}, u32[]{:S(2)}, u32[]{:S(2)}) collective-permute-start(bf16[640,640]{1,0:T(8,128)(2,1)} %rest_0_.1), channel_id=1, source_target_pairs={{16,32},{48,64},{80,96},{112,128},{144,160},{176,192},{208,224},{2... | collective-permute-start | bytes 2457608 | tf_op jit(solution)/shard_map/ppermute | solution.py:108
  8.2 0.9 copy-start.1
  17.9 0.9 copy-start.4
  102.4 5.3 %copy-start = (bf16[640,640]{1,0:T(8,128)(2,1)}, bf16[640,640]{1,0:T(8,128)(2,1)S(1)}, u32[]{:S(2)}) copy-start(bf16[640,640]{1,0:T(8,128)(2,1)S(1)} %all-reduce.2.own) | copy-start | bytes 2457604
  102.4 5.3 %collective-permute-start.2 = (bf16[640,640]{1,0:T(8,128)(2,1)S(1)}, bf16[640,640]{1,0:T(8,128)(2,1)S(1)}, u32[]{:S(2)}, u32[]{:S(2)}) collective-permute-start(bf16[640,640]{1,0:T(8,128)(2,1)S(1)} %all-reduce.2.own), channel_id=1, source_target_pairs={{0,16},{16,0},{32,48},{48,32},{64,80},{80,64},{96,112},{112,96},{1... | collective-permute-start | bytes 2457608 | tf_op jit(solution)/shard_map/ppermute | solution.py:109
  104.4 15.8 %collective-permute-start.3 = (bf16[640,640]{1,0:T(8,128)(2,1)S(1)}, bf16[640,640]{1,0:T(8,128)(2,1)S(1)}, u32[]{:S(2)}, u32[]{:S(2)}) collective-permute-start(bf16[640,640]{1,0:T(8,128)(2,1)S(1)} %all-reduce.2.own), channel_id=1, source_target_pairs={{16,32},{48,64},{80,96},{112,128},{144,160},{176,192},{208,224},{2... | collective-permute-start | bytes 2457608 | tf_op jit(solution)/shard_map/ppermute | solution.py:108
  107.8 0.9 copy-start.3
  120.1 0.9 copy-start.2

commit v4 on v2

v4 whole, which is shorter than its diff:
```python
import jax
import jax.numpy as jnp
from jax import lax
from jax.sharding import PartitionSpec as P


def keep_live(values, live_width):
    row_index = lax.broadcasted_iota(jnp.int32, values.shape, 0)
    col_index = lax.broadcasted_iota(jnp.int32, values.shape, 1)
    return jnp.where(
        (row_index < live_width) & (col_index < live_width), values, jnp.zeros_like(values)
    )


def dot(a, b):
    return jnp.dot(a, b, preferred_element_type=jnp.float32)


def shards(blocks, left_env, right_env, coupling, widths):
    side = blocks.shape[1]
    left_part = left_env[0, 0]
    right_part = right_env[0, 0]
    coupled = coupling[0].astype(jnp.bfloat16)
    live_width = widths[0]
    count = lax.axis_size("sector")
    mate_at = jnp.where(lax.axis_index("sector") % 2 == 0, 2, 0).astype(jnp.int32)
    once = jnp.where(lax.axis_index("term") == 0, 1.0, 0.0)
    across = [(i, i + 1) for i in range(1, count - 1, 2)]
    across += [(j, i) for i, j in across]
    within = [(i, i ^ 1) for i in range(count)]

    def left_of(at):
        piece = lax.dynamic_slice(left_part, (0, at * side), (side, side))
        return piece * lax.dynamic_index_in_dim(coupled, at, keepdims=False)

    left_near = jnp.concatenate([left_of(1), left_of(mate_at)], axis=1)
    left_far = left_of(2 - mate_at)
    left_near, left_far = lax.optimization_barrier((left_near, left_far))

    def live_part(source):
        far = lax.ppermute(source, "sector", across)
        mate = lax.ppermute(source, "sector", within)
        early = dot(left_near, jnp.concatenate([source, mate], axis=0))
        early = lax.optimization_barrier(early)
        partial = (early + dot(left_far, far)).astype(jnp.bfloat16)
        return keep_live(dot(partial, right_part), live_width)

    first_pass = lax.psum(live_part(blocks), "term").astype(jnp.bfloat16)
    second = 2.0 * live_part(first_pass) - once * blocks.astype(jnp.float32)
    return lax.psum(second, "term").astype(jnp.bfloat16)


def solution(mesh):
    placed = (
        P("sector", None),
        P("sector", "term", None, None),
        P("sector", "term", None, None),
        P("sector", None),
        P("sector"),
    )
    return jax.shard_map(
        shards, mesh=mesh, in_specs=placed, out_specs=P("sector", None), check_vma=False
    )
```

time: 201 us -> 195 us (0.970)
  the two profiles are of different devices: /device:TPU:6 before, /device:TPU:24 now
where the time goes in v4:
time: 195 us
  blocking collectives  150 us (77%)
  matrix products  15.7 us (8%)
  starting transfers between devices  12.6 us (6%)
  waiting for transfers between devices  8.37 us (4%)
  other arithmetic  5.63 us (3%)
    psum x1, blocking collectives, shards(): first_pass = lax.psum(live_part(blocks), 'term').astype(jnp.bfloat16)  79 us
    psum x1, blocking collectives, shards(): return lax.psum(second, 'term').astype(jnp.bfloat16)  71.1 us
    dot_general x4, matrix products, dot(): return jnp.dot(a, b, preferred_element_type=jnp.float32)  15.7 us
    ppermute x2, starting transfers between devices, live_part(): far = lax.ppermute(source, 'sector', across)  8.65 us
    ppermute x2, waiting for transfers between devices, live_part(): far = lax.ppermute(source, 'sector', across)  8.36 us
    mul x2, other arithmetic, left_of(): return piece * lax.dynamic_index_in_dim(coupled, at, keepdims=False)  4.85 us
    ppermute x2, starting transfers between devices, live_part(): mate = lax.ppermute(source, 'sector', within)  3.95 us
  transfers between devices with their start and end apart: 4, of which 1 were waited for; matrix products, arithmetic and copies ran while one was open for 7% of the time, Pallas kernels for 0%

profile of v4, /device:TPU:24, one launch (start us, length us, event | category | flops | bytes accessed | tf_op | source)
XLA Modules:
  0.0 194.8 jit_solution(5040967705129091556)
XLA Ops:
  0.0 0.0 copy-start
  0.0 2.0 %collective-permute-start = (bf16[640,640]{1,0:T(8,128)(2,1)}, bf16[640,640]{1,0:T(8,128)(2,1)}, u32[]{:S(2)}, u32[]{:S(2)}) collective-permute-start(bf16[640,640]{1,0:T(8,128)(2,1)} %param.5), channel_id=1, source_target_pairs={{0,16},{16,0},{32,48},{48,32},{64,80},{80,64},{96,112},{112,96},{1... | collective-permute-start | bytes 2457608 | tf_op jit(solution)/shard_map/ppermute | solution.py:42
  2.1 5.0 %collective-permute-start.1 = (bf16[640,640]{1,0:T(8,128)(2,1)}, bf16[640,640]{1,0:T(8,128)(2,1)}, u32[]{:S(2)}, u32[]{:S(2)}) collective-permute-start(bf16[640,640]{1,0:T(8,128)(2,1)} %param.5), channel_id=1, source_target_pairs={{16,32},{48,64},{80,96},{112,128},{144,160},{176,192},{208,224},{2... | collective-permute-start | bytes 2457608 | tf_op jit(solution)/shard_map/ppermute | solution.py:41
  7.7 0.7 convert_element_type.19
  8.3 0.6 constant_dynamic-slice_fusion
  8.9 1.9 slice_multiply_fusion
  10.8 3.0 %multiply_bitcast_fusion = (bf16[640,640]{1,0:T(8,128)(2,1)S(1)}, bf16[640,640]{1,0:T(8,128)(2,1)S(1)}) fusion(bf16[1,1,640,1920]{3,2,1,0:T(8,128)(2,1)} %param.6, s32[]{:T(128)S(6)} %select_n.38, bf16[]{:T(256)} %bitcast.5, bf16[]{:T(256)} %bitcast.3, s32[]{:T(128)S(6)} %select_n.37), kind=kLoop, calls=%fused_computation.18 | loop fusion | flops 3276800 | bytes 3276812 | tf_op jit(solution)/shard_map/mul | solution.py:34
  13.8 0.0 copy-start.1
  13.8 0.1 pad_maximum_fusion
  14.0 0.0 collective-permute-done
  14.0 1.0 copy-done.1
  14.9 3.8 %fusion.2 = f32[640,640]{1,0:T(8,128)} fusion(bf16[640,1280]{1,0:T(8,128)(2,1)S(1)} %pad_maximum_fusion, bf16[640,640]{1,0:T(8,128)(2,1)} %collective-permute-done, bf16[640,640]{1,0:T(8,128)(2,1)S(1)} %copy-done.1), kind=kOutput, calls=%fused_computation.5 | convolution fusion | flops 1051852800 | bytes 4915200 | tf_op jit(solution)/shard_map/dot_general | solution.py:16
  18.7 0.0 collective-permute-done.1
  18.7 0.0 copy-done
  18.7 4.5 %and_select_fusion.1 = f32[640,640]{1,0:T(8,128)} fusion(f32[640,640]{1,0:T(8,128)} %fusion.2, bf16[1,1,640,640]{3,2,1,0:T(8,128)(2,1)S(1)} %copy-done, pred[640]{0:T(1024)(128)(4,1)S(1)} %iota_compare_fusion, bf16[640,640]{1,0:T(8,128)(2,1)S(1)} %get-tuple-element.8, bf16[640,640]{1,0:T(8,128)(2,1)} %collective-permute-done.1), kind=kOutput, calls=%fused_computation.1 | convolution fusion | flops 1050214400 | bytes 5735040 | tf_op jit(solution)/shard_map/dot_general | solution.py:16
  23.2 79.0 %all-reduce.2 = bf16[640,640]{1,0:T(8,128)(2,1)} all-reduce(f32[640,640]{1,0:T(8,128)} %and_select_fusion.1), channel_id=1, replica_groups=mesh['sector'=32,'term'=16] {'term'}, use_global_device_ids=true, to_apply=%region_0.1 | all-reduce | flops 409600 | bytes 2457600 | tf_op jit(solution)/shard_map/psum | solution.py:48
  102.2 1.9 collective-permute-start.2
  104.1 3.7 %collective-permute-start.3 = (bf16[640,640]{1,0:T(8,128)(2,1)}, bf16[640,640]{1,0:T(8,128)(2,1)}, u32[]{:S(2)}, u32[]{:S(2)}) collective-permute-start(bf16[640,640]{1,0:T(8,128)(2,1)} %all-reduce.2), channel_id=1, source_target_pairs={{16,32},{48,64},{80,96},{112,128},{144,160},{176,192},{208,224},{2... | collective-permute-start | bytes 2457608 | tf_op jit(solution)/shard_map/ppermute | solution.py:41
  107.8 0.0 collective-permute-done.2
  107.8 4.0 %fusion.6 = f32[640,640]{1,0:T(8,128)} fusion(bf16[640,1280]{1,0:T(8,128)(2,1)S(1)} %pad_maximum_fusion, bf16[640,640]{1,0:T(8,128)(2,1)} %collective-permute-done.2, bf16[640,640]{1,0:T(8,128)(2,1)} %all-reduce.2), kind=kOutput, calls=%fused_computation.9 | convolution fusion | flops 1051852800 | bytes 4915200 | tf_op jit(solution)/shard_map/dot_general | solution.py:16
  111.8 8.4 %collective-permute-done.3 = bf16[640,640]{1,0:T(8,128)(2,1)} collective-permute-done((bf16[640,640]{1,0:T(8,128)(2,1)}, bf16[640,640]{1,0:T(8,128)(2,1)}, u32[]{:S(2)}, u32[]{:S(2)}) %collective-permute-start.3) | collective-permute-done | bytes 819232 | tf_op jit(solution)/shard_map/ppermute | solution.py:41
  120.2 3.5 %fusion.1 = f32[640,640]{1,0:T(8,128)S(1)} fusion(bf16[640,640]{1,0:T(8,128)(2,1)} %param.5, f32[640,640]{1,0:T(8,128)} %fusion.6, bf16[1,1,640,640]{3,2,1,0:T(8,128)(2,1)S(1)} %copy-done, f32[]{:T(128)S(6)} %select_n.42, pred[640]{0:T(1024)(128)(4,1)S(1)} %iota_compare_fusion, bf16[640,640]{1,0:T(8,128)(2,1)S(1)} %get-tuple-element.8, ...), kind=kOutput, calls=%fused_computation.3 | convolution fusion | flops 1051852800 | bytes 6554244 | tf_op jit(solution)/shard_map/dot_general | solution.py:16
  123.7 71.1 %all-reduce.3 = bf16[640,640]{1,0:T(8,128)(2,1)} all-reduce(f32[640,640]{1,0:T(8,128)S(1)} %fusion.1), channel_id=1, replica_groups=mesh['sector'=32,'term'=16] {'term'}, use_global_device_ids=true, to_apply=%region_1.2 | all-reduce | flops 409600 | bytes 2457600 | tf_op jit(solution)/shard_map/psum | solution.py:50
  (1 shorter events, 0.0 us)
Async XLA Ops:
  0.0 18.7 %copy-start = (bf16[1,1,640,640]{3,2,1,0:T(8,128)(2,1)S(1)}, bf16[1,1,640,640]{3,2,1,0:T(8,128)(2,1)}, u32[]{:S(2)}) copy-start(bf16[1,1,640,640]{3,2,1,0:T(8,128)(2,1)} %param.7) | copy-start | bytes 2457604
  0.0 14.0 %collective-permute-start = (bf16[640,640]{1,0:T(8,128)(2,1)}, bf16[640,640]{1,0:T(8,128)(2,1)}, u32[]{:S(2)}, u32[]{:S(2)}) collective-permute-start(bf16[640,640]{1,0:T(8,128)(2,1)} %param.5), channel_id=1, source_target_pairs={{0,16},{16,0},{32,48},{48,32},{64,80},{80,64},{96,112},{112,96},{1... | collective-permute-start | bytes 2457608 | tf_op jit(solution)/shard_map/ppermute | solution.py:42
  2.1 16.7 %collective-permute-start.1 = (bf16[640,640]{1,0:T(8,128)(2,1)}, bf16[640,640]{1,0:T(8,128)(2,1)}, u32[]{:S(2)}, u32[]{:S(2)}) collective-permute-start(bf16[640,640]{1,0:T(8,128)(2,1)} %param.5), channel_id=1, source_target_pairs={{16,32},{48,64},{80,96},{112,128},{144,160},{176,192},{208,224},{2... | collective-permute-start | bytes 2457608 | tf_op jit(solution)/shard_map/ppermute | solution.py:41
  13.8 1.1 copy-start.1
  102.2 5.6 %collective-permute-start.2 = (bf16[640,640]{1,0:T(8,128)(2,1)}, bf16[640,640]{1,0:T(8,128)(2,1)}, u32[]{:S(2)}, u32[]{:S(2)}) collective-permute-start(bf16[640,640]{1,0:T(8,128)(2,1)} %all-reduce.2), channel_id=1, source_target_pairs={{0,16},{16,0},{32,48},{48,32},{64,80},{80,64},{96,112},{112,96},{1... | collective-permute-start | bytes 2457608 | tf_op jit(solution)/shard_map/ppermute | solution.py:42
  104.1 16.1 %collective-permute-start.3 = (bf16[640,640]{1,0:T(8,128)(2,1)}, bf16[640,640]{1,0:T(8,128)(2,1)}, u32[]{:S(2)}, u32[]{:S(2)}) collective-permute-start(bf16[640,640]{1,0:T(8,128)(2,1)} %all-reduce.2), channel_id=1, source_target_pairs={{16,32},{48,64},{80,96},{112,128},{144,160},{176,192},{208,224},{2... | collective-permute-start | bytes 2457608 | tf_op jit(solution)/shard_map/ppermute | solution.py:41

commit v5 on v4

--- a/solution.py
+++ b/solution.py
@@ -1,6 +1,8 @@
 import jax
 import jax.numpy as jnp
 from jax import lax
+from jax.experimental import pallas as pl
+from jax.experimental.pallas import tpu as pltpu
 from jax.sharding import PartitionSpec as P
 
 
@@ -16,32 +18,66 @@
     return jnp.dot(a, b, preferred_element_type=jnp.float32)
 
 
+def mate_place():
+    return 2 - 2 * (lax.axis_index("sector") % 2)
+
+
+CUT_STEPS = 5
+
+
+def cut_body(coupled, left, near, far):
+    side = far.shape[1]
+    mate_first = mate_place() == 0
+
+    def piece(at):
+        scale = coupled[at].astype(jnp.float32)
+        columns = left[:, at * side : (at + 1) * side].astype(jnp.float32)
+        return (columns * scale).astype(left.dtype)
+
+    before, after = piece(0), piece(2)
+    near[:, :side] = piece(1)
+    near[:, side:] = jnp.where(mate_first, before, after)
+    far[...] = jnp.where(mate_first, after, before)
+
+
+def cut(left_part, coupled):
+    side, width = left_part.shape
+    rows = side // CUT_STEPS
+
+    def by_rows(columns):
+        return pl.BlockSpec((rows, columns), lambda i, coupled: (i, 0))
+
+    return pl.pallas_call(
+        cut_body,
+        grid_spec=pltpu.PrefetchScalarGridSpec(
+            num_scalar_prefetch=1,
+            grid=(CUT_STEPS,),
+            in_specs=[by_rows(width)],
+            out_specs=(by_rows(2 * side), by_rows(side)),
+        ),
+        out_shape=(
+            jax.ShapeDtypeStruct((side, 2 * side), left_part.dtype),
+            jax.ShapeDtypeStruct((side, side), left_part.dtype),
+        ),
+        name="cut",
+    )(coupled, left_part)
+
+
 def shards(blocks, left_env, right_env, coupling, widths):
-    side = blocks.shape[1]
-    left_part = left_env[0, 0]
     right_part = right_env[0, 0]
-    coupled = coupling[0].astype(jnp.bfloat16)
     live_width = widths[0]
     count = lax.axis_size("sector")
-    mate_at = jnp.where(lax.axis_index("sector") % 2 == 0, 2, 0).astype(jnp.int32)
     once = jnp.where(lax.axis_index("term") == 0, 1.0, 0.0)
     across = [(i, i + 1) for i in range(1, count - 1, 2)]
     across += [(j, i) for i, j in across]
     within = [(i, i ^ 1) for i in range(count)]
-
-    def left_of(at):
-        piece = lax.dynamic_slice(left_part, (0, at * side), (side, side))
-        return piece * lax.dynamic_index_in_dim(coupled, at, keepdims=False)
-
-    left_near = jnp.concatenate([left_of(1), left_of(mate_at)], axis=1)
-    left_far = left_of(2 - mate_at)
-    left_near, left_far = lax.optimization_barrier((left_near, left_far))
+    left_near, left_far = cut(left_env[0, 0], coupling[0])
 
     def live_part(source):
         far = lax.ppermute(source, "sector", across)
         mate = lax.ppermute(source, "sector", within)
-        early = dot(left_near, jnp.concatenate([source, mate], axis=0))
-        early = lax.optimization_barrier(early)
+        near = jnp.concatenate([source, mate], axis=0)
+        early = lax.optimization_barrier(dot(left_near, near))
         partial = (early + dot(left_far, far)).astype(jnp.bfloat16)
         return keep_live(dot(partial, right_part), live_width)
 

time: 195 us -> 193 us (0.990)
  the two profiles are of different devices: /device:TPU:24 before, /device:TPU:8 now
where the time goes in v5:
time: 193 us
  blocking collectives  149 us (77%)
  matrix products  15.3 us (8%)
  starting transfers between devices  11.7 us (6%)
  waiting for transfers between devices  9.77 us (5%)
  Pallas kernels  5.44 us (3%)
    psum x1, blocking collectives, shards(): first_pass = lax.psum(live_part(blocks), 'term').astype(jnp.bfloat16)  77.8 us
    psum x1, blocking collectives, shards(): return lax.psum(second, 'term').astype(jnp.bfloat16)  70.9 us
    dot_general x4, matrix products, dot(): return jnp.dot(a, b, preferred_element_type=jnp.float32)  15.3 us
    ppermute x2, waiting for transfers between devices, live_part(): far = lax.ppermute(source, 'sector', across)  9.77 us
    ppermute x2, starting transfers between devices, live_part(): far = lax.ppermute(source, 'sector', across)  7.76 us
    pallas_call x1, Pallas kernels, cut(): pl.pallas_call(cut_body, grid_spec=pltpu.PrefetchScalarGridSpec(num_scala...  5.44 us
    ppermute x2, starting transfers between devices, live_part(): mate = lax.ppermute(source, 'sector', within)  3.96 us
  transfers between devices with their start and end apart: 4, of which 2 were waited for; matrix products, arithmetic and copies ran while one was open for 4% of the time, Pallas kernels for 3%

profile of v5, /device:TPU:8, one launch (start us, length us, event | category | flops | bytes accessed | tf_op | source)
XLA Modules:
  0.0 192.6 jit_solution(16755793106521527600)
XLA Ops:
  0.0 0.0 copy-start
  0.0 0.0 copy-start.1
  0.0 2.0 %collective-permute-start = (bf16[640,640]{1,0:T(8,128)(2,1)}, bf16[640,640]{1,0:T(8,128)(2,1)S(1)}, u32[]{:S(2)}, u32[]{:S(2)}) collective-permute-start(bf16[640,640]{1,0:T(8,128)(2,1)} %param.5), channel_id=1, source_target_pairs={{0,16},{16,0},{32,48},{48,32},{64,80},{80,64},{96,112},{112,96},{1... | collective-permute-start | bytes 2457608 | tf_op jit(solution)/shard_map/ppermute | solution.py:78
  2.1 4.7 %collective-permute-start.1 = (bf16[640,640]{1,0:T(8,128)(2,1)}, bf16[640,640]{1,0:T(8,128)(2,1)S(1)}, u32[]{:S(2)}, u32[]{:S(2)}) collective-permute-start(bf16[640,640]{1,0:T(8,128)(2,1)} %param.5), channel_id=1, source_target_pairs={{16,32},{48,64},{80,96},{112,128},{144,160},{176,192},{208,224},{2... | collective-permute-start | bytes 2457608 | tf_op jit(solution)/shard_map/ppermute | solution.py:77
  7.4 5.4 %cut.1 = (bf16[640,1280]{1,0:T(8,128)(2,1)}, bf16[640,640]{1,0:T(8,128)(2,1)}) custom-call(s32[3]{0:T(128)} %bitcast.16, bf16[640,1920]{1,0:T(8,128)(2,1)} %bitcast.15), custom_call_target="tpu_custom_call" | custom-call | tf_op jit(solution)/shard_map/cut/pallas_call | solution.py:50
  12.8 0.0 collective-permute-done
  12.8 0.0 copy-done.1
  12.8 4.1 %fusion.2 = f32[640,640]{1,0:T(8,128)} fusion(bf16[640,1280]{1,0:T(8,128)(2,1)} %get-tuple-element.7, bf16[640,640]{1,0:T(8,128)(2,1)S(1)} %collective-permute-done, bf16[640,640]{1,0:T(8,128)(2,1)S(1)} %copy-done.1), kind=kOutput, calls=%fused_computation.4 | convolution fusion | flops 1051852800 | bytes 4915200 | tf_op jit(solution)/shard_map/dot_general | solution.py:18
  16.9 1.2 collective-permute-done.1
  18.0 0.0 copy-start.3
  18.0 0.9 copy-done.3
  18.9 0.0 copy-done
  19.0 3.5 %and_select_fusion.1 = f32[640,640]{1,0:T(8,128)S(1)} fusion(f32[640,640]{1,0:T(8,128)} %fusion.2, bf16[1,1,640,640]{3,2,1,0:T(8,128)(2,1)S(1)} %copy-done, pred[640]{0:T(1024)(128)(4,1)S(1)} %iota_compare_fusion, bf16[640,640]{1,0:T(8,128)(2,1)} %get-tuple-element.8, bf16[640,640]{1,0:T(8,128)(2,1)} %copy-done.3), kind=kOutput, calls=%fused_computation.1 | convolution fusion | flops 1050214400 | bytes 5735040 | tf_op jit(solution)/shard_map/dot_general | solution.py:18
  22.5 77.8 %all-reduce.2 = bf16[640,640]{1,0:T(8,128)(2,1)S(1)} all-reduce(f32[640,640]{1,0:T(8,128)S(1)} %and_select_fusion.1), channel_id=1, replica_groups=mesh['sector'=32,'term'=16] {'term'}, use_global_device_ids=true, to_apply=%region_0.1 | all-reduce | flops 409600 | bytes 2457600 | tf_op jit(solution)/shard_map/psum | solution.py:84
  100.3 1.9 collective-permute-start.2
  102.2 3.1 %collective-permute-start.3 = (bf16[640,640]{1,0:T(8,128)(2,1)S(1)}, bf16[640,640]{1,0:T(8,128)(2,1)}, u32[]{:S(2)}, u32[]{:S(2)}) collective-permute-start(bf16[640,640]{1,0:T(8,128)(2,1)S(1)} %all-reduce.2), channel_id=1, source_target_pairs={{16,32},{48,64},{80,96},{112,128},{144,160},{176,192},{208,224},{2... | collective-permute-start | bytes 2457608 | tf_op jit(solution)/shard_map/ppermute | solution.py:77
  105.3 0.0 copy-start.2
  105.3 0.0 collective-permute-done.2
  105.3 4.1 %fusion.6 = f32[640,640]{1,0:T(8,128)} fusion(bf16[640,1280]{1,0:T(8,128)(2,1)} %get-tuple-element.7, bf16[640,640]{1,0:T(8,128)(2,1)S(1)} %collective-permute-done.2, bf16[640,640]{1,0:T(8,128)(2,1)S(1)} %all-reduce.2), kind=kOutput, calls=%fused_computation.8 | convolution fusion | flops 1051852800 | bytes 4915200 | tf_op jit(solution)/shard_map/dot_general | solution.py:18
  109.5 8.6 %collective-permute-done.3 = bf16[640,640]{1,0:T(8,128)(2,1)} collective-permute-done((bf16[640,640]{1,0:T(8,128)(2,1)S(1)}, bf16[640,640]{1,0:T(8,128)(2,1)}, u32[]{:S(2)}, u32[]{:S(2)}) %collective-permute-start.3) | collective-permute-done | bytes 819232 | tf_op jit(solution)/shard_map/ppermute | solution.py:77
  118.1 0.0 copy-done.2
  118.1 3.6 %fusion.1 = f32[640,640]{1,0:T(8,128)S(1)} fusion(bf16[640,640]{1,0:T(8,128)(2,1)S(1)} %copy-done.2, f32[640,640]{1,0:T(8,128)} %fusion.6, bf16[1,1,640,640]{3,2,1,0:T(8,128)(2,1)S(1)} %copy-done, f32[]{:T(128)S(6)} %select_n.13, pred[640]{0:T(1024)(128)(4,1)S(1)} %iota_compare_fusion, bf16[640,640]{1,0:T(8,128)(2,1)} %get-tuple-element.8, ...), kind=kOutput, calls=%fused_computation.3 | convolution fusion | flops 1051852800 | bytes 6554244 | tf_op jit(solution)/shard_map/dot_general | solution.py:18
  121.6 70.9 %all-reduce.3 = bf16[640,640]{1,0:T(8,128)(2,1)} all-reduce(f32[640,640]{1,0:T(8,128)S(1)} %fusion.1), channel_id=1, replica_groups=mesh['sector'=32,'term'=16] {'term'}, use_global_device_ids=true, to_apply=%region_1.2 | all-reduce | flops 409600 | bytes 2457600 | tf_op jit(solution)/shard_map/psum | solution.py:86
  (1 shorter events, 0.0 us)
Async XLA Ops:
  0.0 19.0 %copy-start = (bf16[1,1,640,640]{3,2,1,0:T(8,128)(2,1)S(1)}, bf16[1,1,640,640]{3,2,1,0:T(8,128)(2,1)}, u32[]{:S(2)}) copy-start(bf16[1,1,640,640]{3,2,1,0:T(8,128)(2,1)} %param.7) | copy-start | bytes 2457604
  0.0 12.8 %copy-start.1 = (bf16[640,640]{1,0:T(8,128)(2,1)S(1)}, bf16[640,640]{1,0:T(8,128)(2,1)}, u32[]{:S(2)}) copy-start(bf16[640,640]{1,0:T(8,128)(2,1)} %param.5) | copy-start | bytes 2457604
  0.0 12.8 %collective-permute-start = (bf16[640,640]{1,0:T(8,128)(2,1)}, bf16[640,640]{1,0:T(8,128)(2,1)S(1)}, u32[]{:S(2)}, u32[]{:S(2)}) collective-permute-start(bf16[640,640]{1,0:T(8,128)(2,1)} %param.5), channel_id=1, source_target_pairs={{0,16},{16,0},{32,48},{48,32},{64,80},{80,64},{96,112},{112,96},{1... | collective-permute-start | bytes 2457608 | tf_op jit(solution)/shard_map/ppermute | solution.py:78
  2.1 16.0 %collective-permute-start.1 = (bf16[640,640]{1,0:T(8,128)(2,1)}, bf16[640,640]{1,0:T(8,128)(2,1)S(1)}, u32[]{:S(2)}, u32[]{:S(2)}) collective-permute-start(bf16[640,640]{1,0:T(8,128)(2,1)} %param.5), channel_id=1, source_target_pairs={{16,32},{48,64},{80,96},{112,128},{144,160},{176,192},{208,224},{2... | collective-permute-start | bytes 2457608 | tf_op jit(solution)/shard_map/ppermute | solution.py:77
  18.0 0.9 copy-start.3
  100.3 5.1 %collective-permute-start.2 = (bf16[640,640]{1,0:T(8,128)(2,1)S(1)}, bf16[640,640]{1,0:T(8,128)(2,1)S(1)}, u32[]{:S(2)}, u32[]{:S(2)}) collective-permute-start(bf16[640,640]{1,0:T(8,128)(2,1)S(1)} %all-reduce.2), channel_id=1, source_target_pairs={{0,16},{16,0},{32,48},{48,32},{64,80},{80,64},{96,112},{112,96},{1... | collective-permute-start | bytes 2457608 | tf_op jit(solution)/shard_map/ppermute | solution.py:78
  102.2 15.9 %collective-permute-start.3 = (bf16[640,640]{1,0:T(8,128)(2,1)S(1)}, bf16[640,640]{1,0:T(8,128)(2,1)}, u32[]{:S(2)}, u32[]{:S(2)}) collective-permute-start(bf16[640,640]{1,0:T(8,128)(2,1)S(1)} %all-reduce.2), channel_id=1, source_target_pairs={{16,32},{48,64},{80,96},{112,128},{144,160},{176,192},{208,224},{2... | collective-permute-start | bytes 2457608 | tf_op jit(solution)/shard_map/ppermute | solution.py:77
  105.3 12.8 %copy-start.2 = (bf16[640,640]{1,0:T(8,128)(2,1)S(1)}, bf16[640,640]{1,0:T(8,128)(2,1)}, u32[]{:S(2)}) copy-start(bf16[640,640]{1,0:T(8,128)(2,1)} %param.5) | copy-start | bytes 2457604

commit v6 on v5

--- a/solution.py
+++ b/solution.py
@@ -23,21 +23,20 @@
 
 
 CUT_STEPS = 5
+FIRST_ROWS = 384
 
 
 def cut_body(coupled, left, near, far):
     side = far.shape[1]
-    mate_first = mate_place() == 0
+    mate_at = mate_place()
 
     def piece(at):
-        scale = coupled[at].astype(jnp.float32)
-        columns = left[:, at * side : (at + 1) * side].astype(jnp.float32)
-        return (columns * scale).astype(left.dtype)
+        scale = jnp.full((1, side), coupled[at].astype(jnp.float32)).astype(left.dtype)
+        return left[:, pl.ds(pl.multiple_of(at * side, 128), side)] * scale
 
-    before, after = piece(0), piece(2)
     near[:, :side] = piece(1)
-    near[:, side:] = jnp.where(mate_first, before, after)
-    far[...] = jnp.where(mate_first, after, before)
+    near[:, side:] = piece(mate_at)
+    far[...] = piece(2 - mate_at)
 
 
 def cut(left_part, coupled):
@@ -73,16 +72,25 @@
     within = [(i, i ^ 1) for i in range(count)]
     left_near, left_far = cut(left_env[0, 0], coupling[0])
 
-    def live_part(source):
-        far = lax.ppermute(source, "sector", across)
+    def live_part(source, split):
+        far = [None, None]
+        far[0] = lax.ppermute(source[:split], "sector", across)
+        if split < source.shape[0]:
+            far[1] = lax.ppermute(source[split:], "sector", across)
         mate = lax.ppermute(source, "sector", within)
         near = jnp.concatenate([source, mate], axis=0)
         early = lax.optimization_barrier(dot(left_near, near))
-        partial = (early + dot(left_far, far)).astype(jnp.bfloat16)
+        left_last = left_far
+        if far[1] is not None:
+            early, first = lax.optimization_barrier((early, far[0]))
+            early += lax.optimization_barrier(dot(left_far[:, :split], first))
+            left_last = left_far[:, split:]
+        last = far[0] if far[1] is None else far[1]
+        partial = (early + dot(left_last, last)).astype(jnp.bfloat16)
         return keep_live(dot(partial, right_part), live_width)
 
-    first_pass = lax.psum(live_part(blocks), "term").astype(jnp.bfloat16)
-    second = 2.0 * live_part(first_pass) - once * blocks.astype(jnp.float32)
+    first_pass = lax.psum(live_part(blocks, blocks.shape[0]), "term").astype(jnp.bfloat16)
+    second = 2.0 * live_part(first_pass, FIRST_ROWS) - once * blocks.astype(jnp.float32)
     return lax.psum(second, "term").astype(jnp.bfloat16)
 
 

time: 193 us -> 194 us (level)
  the two profiles are of different devices: /device:TPU:8 before, /device:TPU:24 now
where the time goes in v6:
time: 194 us; the launch traced here: 193 us
  blocking collectives  149 us (77%)
  matrix products  17.6 us (9%)
  starting transfers between devices  16.7 us (9%)
  Pallas kernels  5.29 us (3%)
  waiting for transfers between devices  2.1 us (1%)
    psum x1, blocking collectives, shards(): lax.psum(live_part(blocks, blocks.shape[0]), 'term').astype(jnp.bfloat16)  77.7 us
    psum x1, blocking collectives, shards(): return lax.psum(second, 'term').astype(jnp.bfloat16)  71.4 us
    dot_general x5, matrix products, dot(): return jnp.dot(a, b, preferred_element_type=jnp.float32)  17.6 us
    ppermute x2, starting transfers between devices, live_part(): far[0] = lax.ppermute(source[:split], 'sector', across)  8.44 us
    pallas_call x1, Pallas kernels, cut(): pl.pallas_call(cut_body, grid_spec=pltpu.PrefetchScalarGridSpec(num_scala...  5.29 us
    ppermute x1, starting transfers between devices, live_part(): far[1] = lax.ppermute(source[split:], 'sector', across)  4.32 us
    ppermute x2, starting transfers between devices, live_part(): mate = lax.ppermute(source, 'sector', within)  3.96 us
  transfers between devices with their start and end apart: 5, of which 2 were waited for; matrix products, arithmetic and copies ran while one was open for 5% of the time, Pallas kernels for 3%

profile of v6, /device:TPU:24, one launch (start us, length us, event | category | flops | bytes accessed | tf_op | source)
XLA Modules:
  0.0 193.5 jit_solution(11240763375016469528)
XLA Ops:
  0.0 0.0 copy-start
  0.0 0.0 copy-start.3
  0.0 2.0 %collective-permute-start = (bf16[640,640]{1,0:T(8,128)(2,1)}, bf16[640,640]{1,0:T(8,128)(2,1)S(1)}, u32[]{:S(2)}, u32[]{:S(2)}) collective-permute-start(bf16[640,640]{1,0:T(8,128)(2,1)} %param.5), channel_id=1, source_target_pairs={{0,16},{16,0},{32,48},{48,32},{64,80},{80,64},{96,112},{112,96},{1... | collective-permute-start | bytes 2457608 | tf_op jit(solution)/shard_map/ppermute | solution.py:80
  2.1 5.0 %collective-permute-start.1 = (bf16[640,640]{1,0:T(8,128)(2,1)}, bf16[640,640]{1,0:T(8,128)(2,1)S(1)}, u32[]{:S(2)}, u32[]{:S(2)}) collective-permute-start(bf16[640,640]{1,0:T(8,128)(2,1)} %param.5), channel_id=1, source_target_pairs={{16,32},{48,64},{80,96},{112,128},{144,160},{176,192},{208,224},{2... | collective-permute-start | bytes 2457608 | tf_op jit(solution)/shard_map/ppermute | solution.py:77
  7.7 5.3 %cut.1 = (bf16[640,1280]{1,0:T(8,128)(2,1)}, bf16[640,640]{1,0:T(8,128)(2,1)}) custom-call(s32[3]{0:T(128)} %bitcast.16, bf16[640,1920]{1,0:T(8,128)(2,1)} %bitcast.15), custom_call_target="tpu_custom_call" | custom-call | tf_op jit(solution)/shard_map/cut/pallas_call | solution.py:49
  13.0 0.0 collective-permute-done
  13.0 0.0 copy-start.5
  13.0 0.9 copy-done.5
  13.9 0.0 copy-done.3
  13.9 0.0 copy-start.1
  13.9 4.3 %fusion.2 = f32[640,640]{1,0:T(8,128)} fusion(bf16[640,1280]{1,0:T(8,128)(2,1)} %get-tuple-element.9, bf16[640,640]{1,0:T(8,128)(2,1)} %copy-done.5, bf16[640,640]{1,0:T(8,128)(2,1)S(1)} %copy-done.3), kind=kOutput, calls=%fused_computation.4 | convolution fusion | flops 1051852800 | bytes 4915200 | tf_op jit(solution)/shard_map/dot_general | solution.py:18
  18.2 0.0 collective-permute-done.1
  18.2 0.0 copy-start.4
  18.2 0.9 copy-done.4
  19.1 0.0 copy-done
  19.1 0.0 copy-done.1
  19.1 3.3 %and_select_fusion.1 = f32[640,640]{1,0:T(8,128)S(1)} fusion(f32[640,640]{1,0:T(8,128)} %fusion.2, bf16[1,1,640,640]{3,2,1,0:T(8,128)(2,1)S(1)} %copy-done, pred[640]{0:T(1024)(128)(4,1)S(1)} %iota_compare_fusion, bf16[640,640]{1,0:T(8,128)(2,1)S(1)} %copy-done.1, bf16[640,640]{1,0:T(8,128)(2,1)} %copy-done.4), kind=kOutput, calls=%fused_computation.1 | convolution fusion | flops 1050214400 | bytes 5735040 | tf_op jit(solution)/shard_map/dot_general | solution.py:18
  22.4 77.7 %all-reduce.2 = bf16[640,640]{1,0:T(8,128)(2,1)S(1)} all-reduce(f32[640,640]{1,0:T(8,128)S(1)} %and_select_fusion.1), channel_id=1, replica_groups=mesh['sector'=32,'term'=16] {'term'}, use_global_device_ids=true, to_apply=%region_0.1 | all-reduce | flops 409600 | bytes 2457600 | tf_op jit(solution)/shard_map/psum | solution.py:92
  100.2 1.9 collective-permute-start.2
  102.1 3.5 %collective-permute-start.3 = (bf16[384,640]{1,0:T(8,128)(2,1)S(1)}, bf16[384,640]{1,0:T(8,128)(2,1)}, u32[]{:S(2)}, u32[]{:S(2)}) collective-permute-start(bf16[384,640]{1,0:T(8,128)(2,1)S(1)} %slice.16), channel_id=1, source_target_pairs={{16,32},{48,64},{80,96},{112,128},{144,160},{176,192},{208,224},{2... | collective-permute-start | bytes 1474568 | tf_op jit(solution)/shard_map/ppermute | solution.py:77
  105.7 0.0 copy-start.2
  105.7 4.3 %collective-permute-start.4 = (bf16[256,640]{1,0:T(8,128)(2,1)S(1)}, bf16[256,640]{1,0:T(8,128)(2,1)}, u32[]{:S(2)}, u32[]{:S(2)}) collective-permute-start(bf16[256,640]{1,0:T(8,128)(2,1)S(1)} %slice.17), channel_id=1, source_target_pairs={{16,32},{48,64},{80,96},{112,128},{144,160},{176,192},{208,224},{2... | collective-permute-start | bytes 983048 | tf_op jit(solution)/shard_map/ppermute | solution.py:79
  110.0 0.0 collective-permute-done.2
  110.0 4.2 %fusion.6 = f32[640,640]{1,0:T(8,128)} fusion(bf16[640,1280]{1,0:T(8,128)(2,1)} %get-tuple-element.9, bf16[640,640]{1,0:T(8,128)(2,1)} %collective-permute-done.2, bf16[640,640]{1,0:T(8,128)(2,1)S(1)} %all-reduce.2), kind=kOutput, calls=%fused_computation.8 | convolution fusion | flops 1051852800 | bytes 4915200 | tf_op jit(solution)/shard_map/dot_general | solution.py:18
  114.3 0.2 collective-permute-done.3
  114.5 0.0 copy-done.2
  114.5 1.6 fusion.14
  116.2 1.9 collective-permute-done.4
  118.0 4.1 %fusion.1 = f32[640,640]{1,0:T(8,128)} fusion(bf16[640,640]{1,0:T(8,128)(2,1)} %param.5, f32[640,640]{1,0:T(8,128)} %fusion.6, f32[640,640]{1,0:T(8,128)S(1)} %fusion.14, bf16[256,640]{1,0:T(8,128)(2,1)} %collective-permute-done.4, bf16[1,1,640,640]{3,2,1,0:T(8,128)(2,1)S(1)} %copy-done, f32[]{:T(128)S(6)} %select_n.13, ...), kind=kOutput, calls=%fused_computation.3 | convolution fusion | flops 737689600 | bytes 7211012 | tf_op jit(solution)/shard_map/dot_general | solution.py:18
  122.1 71.4 %all-reduce.3 = bf16[640,640]{1,0:T(8,128)(2,1)} all-reduce(f32[640,640]{1,0:T(8,128)} %fusion.1), channel_id=1, replica_groups=mesh['sector'=32,'term'=16] {'term'}, use_global_device_ids=true, to_apply=%region_1.2 | all-reduce | flops 409600 | bytes 2457600 | tf_op jit(solution)/shard_map/psum | solution.py:94
  (3 shorter events, 0.1 us)
Async XLA Ops:
  0.0 19.1 %copy-start = (bf16[1,1,640,640]{3,2,1,0:T(8,128)(2,1)S(1)}, bf16[1,1,640,640]{3,2,1,0:T(8,128)(2,1)}, u32[]{:S(2)}) copy-start(bf16[1,1,640,640]{3,2,1,0:T(8,128)(2,1)} %param.7) | copy-start | bytes 2457604
  0.0 13.9 %copy-start.3 = (bf16[640,640]{1,0:T(8,128)(2,1)S(1)}, bf16[640,640]{1,0:T(8,128)(2,1)}, u32[]{:S(2)}) copy-start(bf16[640,640]{1,0:T(8,128)(2,1)} %param.5) | copy-start | bytes 2457604
  0.0 13.0 %collective-permute-start = (bf16[640,640]{1,0:T(8,128)(2,1)}, bf16[640,640]{1,0:T(8,128)(2,1)S(1)}, u32[]{:S(2)}, u32[]{:S(2)}) collective-permute-start(bf16[640,640]{1,0:T(8,128)(2,1)} %param.5), channel_id=1, source_target_pairs={{0,16},{16,0},{32,48},{48,32},{64,80},{80,64},{96,112},{112,96},{1... | collective-permute-start | bytes 2457608 | tf_op jit(solution)/shard_map/ppermute | solution.py:80
  2.1 16.1 %collective-permute-start.1 = (bf16[640,640]{1,0:T(8,128)(2,1)}, bf16[640,640]{1,0:T(8,128)(2,1)S(1)}, u32[]{:S(2)}, u32[]{:S(2)}) collective-permute-start(bf16[640,640]{1,0:T(8,128)(2,1)} %param.5), channel_id=1, source_target_pairs={{16,32},{48,64},{80,96},{112,128},{144,160},{176,192},{208,224},{2... | collective-permute-start | bytes 2457608 | tf_op jit(solution)/shard_map/ppermute | solution.py:77
  13.0 0.9 copy-start.5
  13.9 5.2 %copy-start.1 = (bf16[640,640]{1,0:T(8,128)(2,1)S(1)}, bf16[640,640]{1,0:T(8,128)(2,1)}, u32[]{:S(2)}) copy-start(bf16[640,640]{1,0:T(8,128)(2,1)} %get-tuple-element.10) | copy-start | bytes 2457604
  18.2 0.9 copy-start.4
  100.2 9.9 %collective-permute-start.2 = (bf16[640,640]{1,0:T(8,128)(2,1)S(1)}, bf16[640,640]{1,0:T(8,128)(2,1)}, u32[]{:S(2)}, u32[]{:S(2)}) collective-permute-start(bf16[640,640]{1,0:T(8,128)(2,1)S(1)} %all-reduce.2), channel_id=1, source_target_pairs={{0,16},{16,0},{32,48},{48,32},{64,80},{80,64},{96,112},{112,96},{1... | collective-permute-start | bytes 2457608 | tf_op jit(solution)/shard_map/ppermute | solution.py:80
  102.1 12.4 %collective-permute-start.3 = (bf16[384,640]{1,0:T(8,128)(2,1)S(1)}, bf16[384,640]{1,0:T(8,128)(2,1)}, u32[]{:S(2)}, u32[]{:S(2)}) collective-permute-start(bf16[384,640]{1,0:T(8,128)(2,1)S(1)} %slice.16), channel_id=1, source_target_pairs={{16,32},{48,64},{80,96},{112,128},{144,160},{176,192},{208,224},{2... | collective-permute-start | bytes 1474568 | tf_op jit(solution)/shard_map/ppermute | solution.py:77
  105.7 8.8 %copy-start.2 = (bf16[640,640]{1,0:T(8,128)(2,1)S(1)}, bf16[640,640]{1,0:T(8,128)(2,1)}, u32[]{:S(2)}) copy-start(bf16[640,640]{1,0:T(8,128)(2,1)} %get-tuple-element.10) | copy-start | bytes 2457604
  105.7 12.3 %collective-permute-start.4 = (bf16[256,640]{1,0:T(8,128)(2,1)S(1)}, bf16[256,640]{1,0:T(8,128)(2,1)}, u32[]{:S(2)}, u32[]{:S(2)}) collective-permute-start(bf16[256,640]{1,0:T(8,128)(2,1)S(1)} %slice.17), channel_id=1, source_target_pairs={{16,32},{48,64},{80,96},{112,128},{144,160},{176,192},{208,224},{2... | collective-permute-start | bytes 983048 | tf_op jit(solution)/shard_map/ppermute | solution.py:79

commit v7 on v5

--- a/solution.py
+++ b/solution.py
@@ -25,40 +25,53 @@
 CUT_STEPS = 5
 
 
-def cut_body(coupled, left, near, far):
+def cut_body(coupled, left, near, far, held, arrived, left_us):
     side = far.shape[1]
-    mate_first = mate_place() == 0
+    rows = side // CUT_STEPS
+    mate_at = mate_place()
+    places = (1, mate_at, 2 - mate_at)
+    chunks = [(step, piece) for step in range(CUT_STEPS) for piece in range(len(places))]
 
-    def piece(at):
-        scale = coupled[at].astype(jnp.float32)
-        columns = left[:, at * side : (at + 1) * side].astype(jnp.float32)
-        return (columns * scale).astype(left.dtype)
+    def copy_in(step, piece):
+        at = pl.ds(step * rows, rows)
+        columns = pl.ds(pl.multiple_of(places[piece] * side, 128), side)
+        return pltpu.make_async_copy(
+            left.at[at, columns], held.at[piece, at, :], arrived.at[step, piece]
+        )
 
-    before, after = piece(0), piece(2)
-    near[:, :side] = piece(1)
-    near[:, side:] = jnp.where(mate_first, before, after)
-    far[...] = jnp.where(mate_first, after, before)
+    def copy_out(step, piece):
+        at = pl.ds(step * rows, rows)
+        target = far.at[at, :] if piece == 2 else near.at[at, pl.ds(piece * side, side)]
+        return pltpu.make_async_copy(held.at[piece, at, :], target, left_us.at[step, piece])
+
+    for chunk in chunks:
+        copy_in(*chunk).start()
+    for step, piece in chunks:
+        copy_in(step, piece).wait()
+        at = pl.ds(step * rows, rows)
+        scale = jnp.full((1, side), coupled[places[piece]].astype(jnp.float32))
+        held[piece, at, :] = held[piece, at, :] * scale.astype(held.dtype)
+        copy_out(step, piece).start()
+    for chunk in chunks:
+        copy_out(*chunk).wait()
 
 
 def cut(left_part, coupled):
-    side, width = left_part.shape
-    rows = side // CUT_STEPS
-
-    def by_rows(columns):
-        return pl.BlockSpec((rows, columns), lambda i, coupled: (i, 0))
-
+    side = left_part.shape[0]
+    anywhere = pl.BlockSpec(memory_space=pl.ANY)
     return pl.pallas_call(
         cut_body,
-        grid_spec=pltpu.PrefetchScalarGridSpec(
-            num_scalar_prefetch=1,
-            grid=(CUT_STEPS,),
-            in_specs=[by_rows(width)],
-            out_specs=(by_rows(2 * side), by_rows(side)),
-        ),
+        in_specs=[pl.BlockSpec(memory_space=pltpu.SMEM), anywhere],
+        out_specs=(anywhere, anywhere),
         out_shape=(
             jax.ShapeDtypeStruct((side, 2 * side), left_part.dtype),
             jax.ShapeDtypeStruct((side, side), left_part.dtype),
         ),
+        scratch_shapes=[
+            pltpu.VMEM((3, side, side), left_part.dtype),
+            pltpu.SemaphoreType.DMA((CUT_STEPS, 3)),
+            pltpu.SemaphoreType.DMA((CUT_STEPS, 3)),
+        ],
         name="cut",
     )(coupled, left_part)
 

time: 193 us -> 193 us (level)
  Pallas kernels: 5.44 us -> 3.39 us
  waiting for transfers between devices: 9.77 us -> 11.8 us
    pallas_call x1, Pallas kernels: 5.44 us -> 3.39 us  [cut(): pl.pallas_call(cut_body, in_specs=[pl.BlockSpec(memory_space=pltpu.SMEM),...]
    ppermute x2, waiting for transfers between devices: 9.77 us -> 11.8 us  [live_part(): far = lax.ppermute(source, 'sector', across)]
  transfers between devices with their start and end apart: 4 -> 4, of which waited for: 2 -> 2; matrix products, arithmetic and copies ran while one was open for 4% -> 4% of each run, Pallas kernels for 3% -> 2%
where the time goes in v7:
time: 193 us
  blocking collectives  149 us (77%)
  matrix products  15.3 us (8%)
  waiting for transfers between devices  11.8 us (6%)
  starting transfers between devices  11.7 us (6%)
  Pallas kernels  3.39 us (2%)
    psum x1, blocking collectives, shards(): first_pass = lax.psum(live_part(blocks), 'term').astype(jnp.bfloat16)  77.8 us
    psum x1, blocking collectives, shards(): return lax.psum(second, 'term').astype(jnp.bfloat16)  70.9 us
    dot_general x4, matrix products, dot(): return jnp.dot(a, b, preferred_element_type=jnp.float32)  15.3 us
    ppermute x2, waiting for transfers between devices, live_part(): far = lax.ppermute(source, 'sector', across)  11.8 us
    ppermute x2, starting transfers between devices, live_part(): far = lax.ppermute(source, 'sector', across)  7.76 us
    ppermute x2, starting transfers between devices, live_part(): mate = lax.ppermute(source, 'sector', within)  3.96 us
  transfers between devices with their start and end apart: 4, of which 2 were waited for; matrix products, arithmetic and copies ran while one was open for 4% of the time, Pallas kernels for 2%

profile of v7, /device:TPU:8, one launch (start us, length us, event | category | flops | bytes accessed | tf_op | source)
XLA Modules:
  0.0 192.6 jit_solution(14572597447245019015)
XLA Ops:
  0.0 0.0 copy-start
  0.0 0.0 copy-start.1
  0.0 2.0 %collective-permute-start = (bf16[640,640]{1,0:T(8,128)(2,1)}, bf16[640,640]{1,0:T(8,128)(2,1)S(1)}, u32[]{:S(2)}, u32[]{:S(2)}) collective-permute-start(bf16[640,640]{1,0:T(8,128)(2,1)} %param.5), channel_id=1, source_target_pairs={{0,16},{16,0},{32,48},{48,32},{64,80},{80,64},{96,112},{112,96},{1... | collective-permute-start | bytes 2457608 | tf_op jit(solution)/shard_map/ppermute | solution.py:91
  2.1 4.7 %collective-permute-start.1 = (bf16[640,640]{1,0:T(8,128)(2,1)}, bf16[640,640]{1,0:T(8,128)(2,1)S(1)}, u32[]{:S(2)}, u32[]{:S(2)}) collective-permute-start(bf16[640,640]{1,0:T(8,128)(2,1)} %param.5), channel_id=1, source_target_pairs={{16,32},{48,64},{80,96},{112,128},{144,160},{176,192},{208,224},{2... | collective-permute-start | bytes 2457608 | tf_op jit(solution)/shard_map/ppermute | solution.py:90
  7.4 3.4 %cut.1 = (bf16[640,1280]{1,0:T(8,128)(2,1)}, bf16[640,640]{1,0:T(8,128)(2,1)}) custom-call(s32[3]{0:T(128)} %bitcast.16, bf16[640,1920]{1,0:T(8,128)(2,1)} %bitcast.15), custom_call_target="tpu_custom_call" | custom-call | tf_op jit(solution)/shard_map/cut/pallas_call | solution.py:62
  10.8 0.0 collective-permute-done
  10.8 0.0 copy-done.1
  10.8 4.0 %fusion.2 = f32[640,640]{1,0:T(8,128)} fusion(bf16[640,1280]{1,0:T(8,128)(2,1)} %get-tuple-element.7, bf16[640,640]{1,0:T(8,128)(2,1)S(1)} %collective-permute-done, bf16[640,640]{1,0:T(8,128)(2,1)S(1)} %copy-done.1), kind=kOutput, calls=%fused_computation.4 | convolution fusion | flops 1051852800 | bytes 4915200 | tf_op jit(solution)/shard_map/dot_general | solution.py:18
  14.9 3.2 %collective-permute-done.1 = bf16[640,640]{1,0:T(8,128)(2,1)S(1)} collective-permute-done((bf16[640,640]{1,0:T(8,128)(2,1)}, bf16[640,640]{1,0:T(8,128)(2,1)S(1)}, u32[]{:S(2)}, u32[]{:S(2)}) %collective-permute-start.1) | collective-permute-done | bytes 819232 | tf_op jit(solution)/shard_map/ppermute | solution.py:90
  18.0 0.0 copy-start.3
  18.0 0.9 copy-done.3
  18.9 0.0 copy-done
  19.0 3.5 %and_select_fusion.1 = f32[640,640]{1,0:T(8,128)S(1)} fusion(f32[640,640]{1,0:T(8,128)} %fusion.2, bf16[1,1,640,640]{3,2,1,0:T(8,128)(2,1)S(1)} %copy-done, pred[640]{0:T(1024)(128)(4,1)S(1)} %iota_compare_fusion, bf16[640,640]{1,0:T(8,128)(2,1)} %get-tuple-element.8, bf16[640,640]{1,0:T(8,128)(2,1)} %copy-done.3), kind=kOutput, calls=%fused_computation.1 | convolution fusion | flops 1050214400 | bytes 5735040 | tf_op jit(solution)/shard_map/dot_general | solution.py:18
  22.5 77.8 %all-reduce.2 = bf16[640,640]{1,0:T(8,128)(2,1)S(1)} all-reduce(f32[640,640]{1,0:T(8,128)S(1)} %and_select_fusion.1), channel_id=1, replica_groups=mesh['sector'=32,'term'=16] {'term'}, use_global_device_ids=true, to_apply=%region_0.1 | all-reduce | flops 409600 | bytes 2457600 | tf_op jit(solution)/shard_map/psum | solution.py:97
  100.3 1.9 collective-permute-start.2
  102.2 3.1 %collective-permute-start.3 = (bf16[640,640]{1,0:T(8,128)(2,1)S(1)}, bf16[640,640]{1,0:T(8,128)(2,1)}, u32[]{:S(2)}, u32[]{:S(2)}) collective-permute-start(bf16[640,640]{1,0:T(8,128)(2,1)S(1)} %all-reduce.2), channel_id=1, source_target_pairs={{16,32},{48,64},{80,96},{112,128},{144,160},{176,192},{208,224},{2... | collective-permute-start | bytes 2457608 | tf_op jit(solution)/shard_map/ppermute | solution.py:90
  105.3 0.0 copy-start.2
  105.3 0.0 collective-permute-done.2
  105.3 4.1 %fusion.6 = f32[640,640]{1,0:T(8,128)} fusion(bf16[640,1280]{1,0:T(8,128)(2,1)} %get-tuple-element.7, bf16[640,640]{1,0:T(8,128)(2,1)S(1)} %collective-permute-done.2, bf16[640,640]{1,0:T(8,128)(2,1)S(1)} %all-reduce.2), kind=kOutput, calls=%fused_computation.8 | convolution fusion | flops 1051852800 | bytes 4915200 | tf_op jit(solution)/shard_map/dot_general | solution.py:18
  109.5 8.6 %collective-permute-done.3 = bf16[640,640]{1,0:T(8,128)(2,1)} collective-permute-done((bf16[640,640]{1,0:T(8,128)(2,1)S(1)}, bf16[640,640]{1,0:T(8,128)(2,1)}, u32[]{:S(2)}, u32[]{:S(2)}) %collective-permute-start.3) | collective-permute-done | bytes 819232 | tf_op jit(solution)/shard_map/ppermute | solution.py:90
  118.1 0.0 copy-done.2
  118.1 3.6 %fusion.1 = f32[640,640]{1,0:T(8,128)S(1)} fusion(bf16[640,640]{1,0:T(8,128)(2,1)S(1)} %copy-done.2, f32[640,640]{1,0:T(8,128)} %fusion.6, bf16[1,1,640,640]{3,2,1,0:T(8,128)(2,1)S(1)} %copy-done, f32[]{:T(128)S(6)} %select_n.13, pred[640]{0:T(1024)(128)(4,1)S(1)} %iota_compare_fusion, bf16[640,640]{1,0:T(8,128)(2,1)} %get-tuple-element.8, ...), kind=kOutput, calls=%fused_computation.3 | convolution fusion | flops 1051852800 | bytes 6554244 | tf_op jit(solution)/shard_map/dot_general | solution.py:18
  121.6 70.9 %all-reduce.3 = bf16[640,640]{1,0:T(8,128)(2,1)} all-reduce(f32[640,640]{1,0:T(8,128)S(1)} %fusion.1), channel_id=1, replica_groups=mesh['sector'=32,'term'=16] {'term'}, use_global_device_ids=true, to_apply=%region_1.2 | all-reduce | flops 409600 | bytes 2457600 | tf_op jit(solution)/shard_map/psum | solution.py:99
  (1 shorter events, 0.0 us)
Async XLA Ops:
  0.0 19.0 %copy-start = (bf16[1,1,640,640]{3,2,1,0:T(8,128)(2,1)S(1)}, bf16[1,1,640,640]{3,2,1,0:T(8,128)(2,1)}, u32[]{:S(2)}) copy-start(bf16[1,1,640,640]{3,2,1,0:T(8,128)(2,1)} %param.7) | copy-start | bytes 2457604
  0.0 10.8 %copy-start.1 = (bf16[640,640]{1,0:T(8,128)(2,1)S(1)}, bf16[640,640]{1,0:T(8,128)(2,1)}, u32[]{:S(2)}) copy-start(bf16[640,640]{1,0:T(8,128)(2,1)} %param.5) | copy-start | bytes 2457604
  0.0 10.8 %collective-permute-start = (bf16[640,640]{1,0:T(8,128)(2,1)}, bf16[640,640]{1,0:T(8,128)(2,1)S(1)}, u32[]{:S(2)}, u32[]{:S(2)}) collective-permute-start(bf16[640,640]{1,0:T(8,128)(2,1)} %param.5), channel_id=1, source_target_pairs={{0,16},{16,0},{32,48},{48,32},{64,80},{80,64},{96,112},{112,96},{1... | collective-permute-start | bytes 2457608 | tf_op jit(solution)/shard_map/ppermute | solution.py:91
  2.1 16.0 %collective-permute-start.1 = (bf16[640,640]{1,0:T(8,128)(2,1)}, bf16[640,640]{1,0:T(8,128)(2,1)S(1)}, u32[]{:S(2)}, u32[]{:S(2)}) collective-permute-start(bf16[640,640]{1,0:T(8,128)(2,1)} %param.5), channel_id=1, source_target_pairs={{16,32},{48,64},{80,96},{112,128},{144,160},{176,192},{208,224},{2... | collective-permute-start | bytes 2457608 | tf_op jit(solution)/shard_map/ppermute | solution.py:90
  18.0 0.9 copy-start.3
  100.3 5.1 %collective-permute-start.2 = (bf16[640,640]{1,0:T(8,128)(2,1)S(1)}, bf16[640,640]{1,0:T(8,128)(2,1)S(1)}, u32[]{:S(2)}, u32[]{:S(2)}) collective-permute-start(bf16[640,640]{1,0:T(8,128)(2,1)S(1)} %all-reduce.2), channel_id=1, source_target_pairs={{0,16},{16,0},{32,48},{48,32},{64,80},{80,64},{96,112},{112,96},{1... | collective-permute-start | bytes 2457608 | tf_op jit(solution)/shard_map/ppermute | solution.py:91
  102.2 15.9 %collective-permute-start.3 = (bf16[640,640]{1,0:T(8,128)(2,1)S(1)}, bf16[640,640]{1,0:T(8,128)(2,1)}, u32[]{:S(2)}, u32[]{:S(2)}) collective-permute-start(bf16[640,640]{1,0:T(8,128)(2,1)S(1)} %all-reduce.2), channel_id=1, source_target_pairs={{16,32},{48,64},{80,96},{112,128},{144,160},{176,192},{208,224},{2... | collective-permute-start | bytes 2457608 | tf_op jit(solution)/shard_map/ppermute | solution.py:90
  105.3 12.8 %copy-start.2 = (bf16[640,640]{1,0:T(8,128)(2,1)S(1)}, bf16[640,640]{1,0:T(8,128)(2,1)}, u32[]{:S(2)}) copy-start(bf16[640,640]{1,0:T(8,128)(2,1)} %param.5) | copy-start | bytes 2457604

commit v8 on v7

--- a/solution.py
+++ b/solution.py
@@ -88,9 +88,10 @@
 
     def live_part(source):
         far = lax.ppermute(source, "sector", across)
-        mate = lax.ppermute(source, "sector", within)
-        near = jnp.concatenate([source, mate], axis=0)
-        early = lax.optimization_barrier(dot(left_near, near))
+        side = source.shape[0]
+        early, sent = lax.optimization_barrier((dot(left_near[:, :side], source), source))
+        mate = lax.ppermute(sent, "sector", within)
+        early = lax.optimization_barrier(early + dot(left_near[:, side:], mate))
         partial = (early + dot(left_far, far)).astype(jnp.bfloat16)
         return keep_live(dot(partial, right_part), live_width)
 

time: 193 us -> 202 us (1.047)
  waiting for transfers between devices: 11.8 us -> 17.4 us
  matrix products: 15.3 us -> 18.4 us
    ppermute x2, waiting for transfers between devices: 11.8 us -> 17.4 us  [live_part(): far = lax.ppermute(source, 'sector', across)]
    dot_general x4 -> x6, matrix products: 15.3 us -> 18.4 us  [dot(): return jnp.dot(a, b, preferred_element_type=jnp.float32)]
  transfers between devices with their start and end apart: 4 -> 4, of which waited for: 2 -> 2; matrix products, arithmetic and copies ran while one was open for 4% -> 3% of each run, Pallas kernels for 2% -> 0%
where the time goes in v8:
time: 202 us
  blocking collectives  149 us (74%)
  matrix products  18.4 us (9%)
  waiting for transfers between devices  17.4 us (9%)
  starting transfers between devices  11.6 us (6%)
  Pallas kernels  3.53 us (2%)
    psum x1, blocking collectives, shards(): first_pass = lax.psum(live_part(blocks), 'term').astype(jnp.bfloat16)  78.4 us
    psum x1, blocking collectives, shards(): return lax.psum(second, 'term').astype(jnp.bfloat16)  70.8 us
    dot_general x6, matrix products, dot(): return jnp.dot(a, b, preferred_element_type=jnp.float32)  18.4 us
    ppermute x2, waiting for transfers between devices, live_part(): far = lax.ppermute(source, 'sector', across)  17.4 us
    ppermute x2, starting transfers between devices, live_part(): far = lax.ppermute(source, 'sector', across)  7.76 us
  transfers between devices with their start and end apart: 4, of which 2 were waited for; matrix products, arithmetic and copies ran while one was open for 3% of the time, Pallas kernels for 0%

profile of v8, /device:TPU:8, one launch (start us, length us, event | category | flops | bytes accessed | tf_op | source)
XLA Modules:
  0.0 201.8 jit_solution(10599320305734631785)
XLA Ops:
  0.0 0.0 copy-start
  0.0 0.0 copy-start.2
  0.0 3.5 %cut.1 = (bf16[640,1280]{1,0:T(8,128)(2,1)}, bf16[640,640]{1,0:T(8,128)(2,1)}) custom-call(s32[3]{0:T(128)} %bitcast.18, bf16[640,1920]{1,0:T(8,128)(2,1)} %bitcast.17), custom_call_target="tpu_custom_call" | custom-call | tf_op jit(solution)/shard_map/cut/pallas_call | solution.py:62
  3.5 0.0 copy-done.2
  3.5 0.0 copy-start.1
  3.6 2.1 %fusion.8 = f32[640,640]{1,0:T(8,128)S(1)} fusion(bf16[640,640]{1,0:T(8,128)(2,1)S(1)} %copy-done.2, bf16[640,1280]{1,0:T(8,128)(2,1)} %get-tuple-element.11), kind=kOutput, calls=%fused_computation.14 | convolution fusion | flops 524288000 | bytes 3276800 | tf_op jit(solution)/shard_map/dot_general | solution.py:18
  5.7 1.9 collective-permute-start
  7.6 4.7 %collective-permute-start.1 = (bf16[640,640]{1,0:T(8,128)(2,1)S(1)}, bf16[640,640]{1,0:T(8,128)(2,1)S(1)}, u32[]{:S(2)}, u32[]{:S(2)}) collective-permute-start(bf16[640,640]{1,0:T(8,128)(2,1)S(1)} %copy-done.2), channel_id=1, source_target_pairs={{16,32},{48,64},{80,96},{112,128},{144,160},{176,192},{208,224},{2... | collective-permute-start | bytes 2457608 | tf_op jit(solution)/shard_map/ppermute | solution.py:90
  13.0 0.0 collective-permute-done
  13.0 0.0 copy-done.1
  13.0 2.0 %convolution_add_fusion.1 = f32[640,640]{1,0:T(8,128)} fusion(f32[640,640]{1,0:T(8,128)S(1)} %fusion.8, bf16[640,640]{1,0:T(8,128)(2,1)S(1)} %collective-permute-done, bf16[640,1280]{1,0:T(8,128)(2,1)S(1)} %copy-done.1), kind=kOutput, calls=%fused_computation.7 | convolution fusion | flops 524697600 | bytes 4915200 | tf_op jit(solution)/shard_map/dot_general | solution.py:18
  15.0 8.4 %collective-permute-done.1 = bf16[640,640]{1,0:T(8,128)(2,1)S(1)} collective-permute-done((bf16[640,640]{1,0:T(8,128)(2,1)S(1)}, bf16[640,640]{1,0:T(8,128)(2,1)S(1)}, u32[]{:S(2)}, u32[]{:S(2)}) %collective-permute-start.1) | collective-permute-done | bytes 819232 | tf_op jit(solution)/shard_map/ppermute | solution.py:90
  23.4 0.0 copy-start.3
  23.4 0.9 copy-done.3
  24.3 0.0 copy-done
  24.3 4.7 %and_select_fusion.1 = f32[640,640]{1,0:T(8,128)} fusion(f32[640,640]{1,0:T(8,128)} %convolution_add_fusion.1, bf16[1,1,640,640]{3,2,1,0:T(8,128)(2,1)S(1)} %copy-done, pred[640]{0:T(1024)(128)(4,1)S(1)} %iota_compare_fusion, bf16[640,640]{1,0:T(8,128)(2,1)} %get-tuple-element.14, bf16[640,640]{1,0:T(8,128)(2,1)} %copy-done.3), kind=kOutput, calls=%fused_computation.1 | convolution fusion | flops 1050214400 | bytes 5735040 | tf_op jit(solution)/shard_map/dot_general | solution.py:18
  29.0 78.4 %all-reduce.2 = bf16[640,640]{1,0:T(8,128)(2,1)S(1)} all-reduce(f32[640,640]{1,0:T(8,128)} %and_select_fusion.1), channel_id=1, replica_groups=mesh['sector'=32,'term'=16] {'term'}, use_global_device_ids=true, to_apply=%region_0.1 | all-reduce | flops 409600 | bytes 2457600 | tf_op jit(solution)/shard_map/psum | solution.py:98
  107.5 2.0 %fusion.6 = f32[640,640]{1,0:T(8,128)} fusion(bf16[640,640]{1,0:T(8,128)(2,1)S(1)} %all-reduce.2, bf16[640,1280]{1,0:T(8,128)(2,1)S(1)} %copy-done.1), kind=kOutput, calls=%fused_computation.12 | convolution fusion | flops 524288000 | bytes 3276800 | tf_op jit(solution)/shard_map/dot_general | solution.py:18
  109.5 1.9 collective-permute-start.2
  111.4 3.1 %collective-permute-start.3 = (bf16[640,640]{1,0:T(8,128)(2,1)S(1)}, bf16[640,640]{1,0:T(8,128)(2,1)}, u32[]{:S(2)}, u32[]{:S(2)}) collective-permute-start(bf16[640,640]{1,0:T(8,128)(2,1)S(1)} %all-reduce.2), channel_id=1, source_target_pairs={{16,32},{48,64},{80,96},{112,128},{144,160},{176,192},{208,224},{2... | collective-permute-start | bytes 2457608 | tf_op jit(solution)/shard_map/ppermute | solution.py:90
  114.6 0.0 collective-permute-done.2
  114.6 3.7 %convolution_add_fusion = f32[640,640]{1,0:T(8,128)} fusion(f32[640,640]{1,0:T(8,128)} %fusion.6, bf16[640,640]{1,0:T(8,128)(2,1)} %collective-permute-done.2, bf16[640,1280]{1,0:T(8,128)(2,1)S(1)} %copy-done.1), kind=kOutput, calls=%fused_computation.6 | convolution fusion | flops 524697600 | bytes 4915200 | tf_op jit(solution)/shard_map/dot_general | solution.py:18
  118.3 9.0 %collective-permute-done.3 = bf16[640,640]{1,0:T(8,128)(2,1)} collective-permute-done((bf16[640,640]{1,0:T(8,128)(2,1)S(1)}, bf16[640,640]{1,0:T(8,128)(2,1)}, u32[]{:S(2)}, u32[]{:S(2)}) %collective-permute-start.3) | collective-permute-done | bytes 819232 | tf_op jit(solution)/shard_map/ppermute | solution.py:90
  127.3 3.7 %fusion.1 = f32[640,640]{1,0:T(8,128)S(1)} fusion(bf16[640,640]{1,0:T(8,128)(2,1)} %param.5, f32[640,640]{1,0:T(8,128)} %convolution_add_fusion, bf16[1,1,640,640]{3,2,1,0:T(8,128)(2,1)S(1)} %copy-done, f32[]{:T(128)S(6)} %select_n.13, pred[640]{0:T(1024)(128)(4,1)S(1)} %iota_compare_fusion, bf16[640,640]{1,0:T(8,128)(2,1)} %get-tuple-element.14, ...), kind=kOutput, calls=%fused_computation.3 | convolution fusion | flops 1051852800 | bytes 6554244 | tf_op jit(solution)/shard_map/dot_general | solution.py:18
  131.1 70.8 %all-reduce.3 = bf16[640,640]{1,0:T(8,128)(2,1)} all-reduce(f32[640,640]{1,0:T(8,128)S(1)} %fusion.1), channel_id=1, replica_groups=mesh['sector'=32,'term'=16] {'term'}, use_global_device_ids=true, to_apply=%region_1.2 | all-reduce | flops 409600 | bytes 2457600 | tf_op jit(solution)/shard_map/psum | solution.py:100
  (1 shorter events, 0.0 us)
Async XLA Ops:
  0.0 24.3 %copy-start = (bf16[1,1,640,640]{3,2,1,0:T(8,128)(2,1)S(1)}, bf16[1,1,640,640]{3,2,1,0:T(8,128)(2,1)}, u32[]{:S(2)}) copy-start(bf16[1,1,640,640]{3,2,1,0:T(8,128)(2,1)} %param.7) | copy-start | bytes 2457604
  0.0 3.5 %copy-start.2 = (bf16[640,640]{1,0:T(8,128)(2,1)S(1)}, bf16[640,640]{1,0:T(8,128)(2,1)}, u32[]{:S(2)}) copy-start(bf16[640,640]{1,0:T(8,128)(2,1)} %param.5) | copy-start | bytes 2457604
  3.5 9.4 %copy-start.1 = (bf16[640,1280]{1,0:T(8,128)(2,1)S(1)}, bf16[640,1280]{1,0:T(8,128)(2,1)}, u32[]{:S(2)}) copy-start(bf16[640,1280]{1,0:T(8,128)(2,1)} %get-tuple-element.11) | copy-start | bytes 4915204
  5.7 7.3 %collective-permute-start = (bf16[640,640]{1,0:T(8,128)(2,1)S(1)}, bf16[640,640]{1,0:T(8,128)(2,1)S(1)}, u32[]{:S(2)}, u32[]{:S(2)}) collective-permute-start(bf16[640,640]{1,0:T(8,128)(2,1)S(1)} %copy-done.2), channel_id=1, source_target_pairs={{0,16},{16,0},{32,48},{48,32},{64,80},{80,64},{96,112},{112,96},{1... | collective-permute-start | bytes 2457608 | tf_op jit(solution)/shard_map/ppermute | solution.py:93
  7.6 15.8 %collective-permute-start.1 = (bf16[640,640]{1,0:T(8,128)(2,1)S(1)}, bf16[640,640]{1,0:T(8,128)(2,1)S(1)}, u32[]{:S(2)}, u32[]{:S(2)}) collective-permute-start(bf16[640,640]{1,0:T(8,128)(2,1)S(1)} %copy-done.2), channel_id=1, source_target_pairs={{16,32},{48,64},{80,96},{112,128},{144,160},{176,192},{208,224},{2... | collective-permute-start | bytes 2457608 | tf_op jit(solution)/shard_map/ppermute | solution.py:90
  23.4 0.9 copy-start.3
  109.5 5.0 %collective-permute-start.2 = (bf16[640,640]{1,0:T(8,128)(2,1)S(1)}, bf16[640,640]{1,0:T(8,128)(2,1)}, u32[]{:S(2)}, u32[]{:S(2)}) collective-permute-start(bf16[640,640]{1,0:T(8,128)(2,1)S(1)} %all-reduce.2), channel_id=1, source_target_pairs={{0,16},{16,0},{32,48},{48,32},{64,80},{80,64},{96,112},{112,96},{1... | collective-permute-start | bytes 2457608 | tf_op jit(solution)/shard_map/ppermute | solution.py:93
  111.4 15.9 %collective-permute-start.3 = (bf16[640,640]{1,0:T(8,128)(2,1)S(1)}, bf16[640,640]{1,0:T(8,128)(2,1)}, u32[]{:S(2)}, u32[]{:S(2)}) collective-permute-start(bf16[640,640]{1,0:T(8,128)(2,1)S(1)} %all-reduce.2), channel_id=1, source_target_pairs={{16,32},{48,64},{80,96},{112,128},{144,160},{176,192},{208,224},{2... | collective-permute-start | bytes 2457608 | tf_op jit(solution)/shard_map/ppermute | solution.py:90

commit v9 on v7

--- a/solution.py
+++ b/solution.py
@@ -94,7 +94,10 @@
         partial = (early + dot(left_far, far)).astype(jnp.bfloat16)
         return keep_live(dot(partial, right_part), live_width)
 
-    first_pass = lax.psum(live_part(blocks), "term").astype(jnp.bfloat16)
+    part = live_part(blocks)
+    half = part.shape[0] // 2
+    sums = lax.psum((part[:half], part[half:]), "term")
+    first_pass = jnp.concatenate([half_sum.astype(jnp.bfloat16) for half_sum in sums])
     second = 2.0 * live_part(first_pass) - once * blocks.astype(jnp.float32)
     return lax.psum(second, "term").astype(jnp.bfloat16)
 

time: 193 us -> 194 us (level)
  no operation moved by 1% of the time
where the time goes in v9:
time: 194 us
  blocking collectives  149 us (77%)
  matrix products  16.4 us (8%)
  starting transfers between devices  11.7 us (6%)
  waiting for transfers between devices  10.5 us (5%)
  Pallas kernels  3.39 us (2%)
  local copies, waits for them, and re-layouts  2.42 us (1%)
    psum x1, blocking collectives, shards(): sums = lax.psum((part[:half], part[half:]), 'term')  77.8 us
    psum x1, blocking collectives, shards(): return lax.psum(second, 'term').astype(jnp.bfloat16)  71 us
    dot_general x4, matrix products, dot(): return jnp.dot(a, b, preferred_element_type=jnp.float32)  16.4 us
    ppermute x2, waiting for transfers between devices, live_part(): far = lax.ppermute(source, 'sector', across)  10.5 us
    ppermute x2, starting transfers between devices, live_part(): far = lax.ppermute(source, 'sector', across)  7.75 us
    ppermute x2, starting transfers between devices, live_part(): mate = lax.ppermute(source, 'sector', within)  3.96 us
  transfers between devices with their start and end apart: 4, of which 2 were waited for; matrix products, arithmetic and copies ran while one was open for 4% of the time, Pallas kernels for 2%

profile of v9, /device:TPU:8, one launch (start us, length us, event | category | flops | bytes accessed | tf_op | source)
XLA Modules:
  0.0 194.0 jit_solution(17781579570259491513)
XLA Ops:
  0.0 0.0 copy-start
  0.0 0.0 copy-start.1
  0.0 2.0 %collective-permute-start = (bf16[640,640]{1,0:T(8,128)(2,1)}, bf16[640,640]{1,0:T(8,128)(2,1)S(1)}, u32[]{:S(2)}, u32[]{:S(2)}) collective-permute-start(bf16[640,640]{1,0:T(8,128)(2,1)} %param.5), channel_id=1, source_target_pairs={{0,16},{16,0},{32,48},{48,32},{64,80},{80,64},{96,112},{112,96},{1... | collective-permute-start | bytes 2457608 | tf_op jit(solution)/shard_map/ppermute | solution.py:91
  2.1 4.7 %collective-permute-start.1 = (bf16[640,640]{1,0:T(8,128)(2,1)}, bf16[640,640]{1,0:T(8,128)(2,1)S(1)}, u32[]{:S(2)}, u32[]{:S(2)}) collective-permute-start(bf16[640,640]{1,0:T(8,128)(2,1)} %param.5), channel_id=1, source_target_pairs={{16,32},{48,64},{80,96},{112,128},{144,160},{176,192},{208,224},{2... | collective-permute-start | bytes 2457608 | tf_op jit(solution)/shard_map/ppermute | solution.py:90
  7.4 3.4 %cut.1 = (bf16[640,1280]{1,0:T(8,128)(2,1)}, bf16[640,640]{1,0:T(8,128)(2,1)}) custom-call(s32[3]{0:T(128)} %bitcast.16, bf16[640,1920]{1,0:T(8,128)(2,1)} %bitcast.15), custom_call_target="tpu_custom_call" | custom-call | tf_op jit(solution)/shard_map/cut/pallas_call | solution.py:62
  10.8 0.0 collective-permute-done
  10.8 0.0 copy-start.4
  10.8 0.9 copy-done.4
  11.7 0.0 copy-done.1
  11.7 0.0 copy-start.3
  11.7 4.3 %fusion.2 = f32[640,640]{1,0:T(8,128)} fusion(bf16[640,1280]{1,0:T(8,128)(2,1)} %get-tuple-element.7, bf16[640,640]{1,0:T(8,128)(2,1)} %copy-done.4, bf16[640,640]{1,0:T(8,128)(2,1)S(1)} %copy-done.1), kind=kOutput, calls=%fused_computation.4 | convolution fusion | flops 1051852800 | bytes 4915200 | tf_op jit(solution)/shard_map/dot_general | solution.py:18
  16.0 2.0 %collective-permute-done.1 = bf16[640,640]{1,0:T(8,128)(2,1)S(1)} collective-permute-done((bf16[640,640]{1,0:T(8,128)(2,1)}, bf16[640,640]{1,0:T(8,128)(2,1)S(1)}, u32[]{:S(2)}, u32[]{:S(2)}) %collective-permute-start.1) | collective-permute-done | bytes 819232 | tf_op jit(solution)/shard_map/ppermute | solution.py:90
  18.0 0.0 copy-done
  18.0 0.0 copy-done.3
  18.0 4.2 %and_select_fusion.1 = f32[640,640]{1,0:T(8,128)} fusion(f32[640,640]{1,0:T(8,128)} %fusion.2, bf16[1,1,640,640]{3,2,1,0:T(8,128)(2,1)S(1)} %copy-done, pred[640]{0:T(1024)(128)(4,1)S(1)} %iota_compare_fusion, bf16[640,640]{1,0:T(8,128)(2,1)S(1)} %copy-done.3, bf16[640,640]{1,0:T(8,128)(2,1)S(1)} %collective-permute-done.1), kind=kOutput, calls=%fused_computation.1 | convolution fusion | flops 1050214400 | bytes 5735040 | tf_op jit(solution)/shard_map/dot_general | solution.py:18
  22.3 1.5 fusion.16
  23.8 77.8 %all-reduce.3 = (bf16[320,640]{1,0:T(8,128)(2,1)S(1)}, bf16[320,640]{1,0:T(8,128)(2,1)S(1)}) all-reduce(f32[320,640]{1,0:T(8,128)S(1)} %get-tuple-element.12, f32[320,640]{1,0:T(8,128)S(1)} %get-tuple-element.11), channel_id=1, replica_groups=mesh['sector'=32,'term'=16] {'term'}, use_global_device_ids=true, to_apply=%region_1.2 | all-reduce | flops 409600 | bytes 2457600 | tf_op jit(solution)/shard_map/psum | solution.py:99
  101.6 0.1 pad_maximum_fusion
  101.7 1.9 collective-permute-start.2
  103.6 3.1 %collective-permute-start.3 = (bf16[640,640]{1,0:T(8,128)(2,1)S(1)}, bf16[640,640]{1,0:T(8,128)(2,1)}, u32[]{:S(2)}, u32[]{:S(2)}) collective-permute-start(bf16[640,640]{1,0:T(8,128)(2,1)S(1)} %pad_maximum_fusion), channel_id=1, source_target_pairs={{16,32},{48,64},{80,96},{112,128},{144,160},{176,192},{208,224},{2... | collective-permute-start | bytes 2457608 | tf_op jit(solution)/shard_map/ppermute | solution.py:90
  106.7 0.0 copy-start.2
  106.7 0.0 collective-permute-done.2
  106.7 4.3 %fusion.6 = f32[640,640]{1,0:T(8,128)} fusion(bf16[640,1280]{1,0:T(8,128)(2,1)} %get-tuple-element.7, bf16[640,640]{1,0:T(8,128)(2,1)} %collective-permute-done.2, bf16[320,640]{1,0:T(8,128)(2,1)S(1)} %get-tuple-element.9, bf16[320,640]{1,0:T(8,128)(2,1)S(1)} %get-tuple-element.10), kind=kOutput, calls=%fused_computation.8 | convolution fusion | flops 1053491200 | bytes 4915200 | tf_op jit(solution)/shard_map/dot_general | solution.py:18
  111.0 8.4 %collective-permute-done.3 = bf16[640,640]{1,0:T(8,128)(2,1)} collective-permute-done((bf16[640,640]{1,0:T(8,128)(2,1)S(1)}, bf16[640,640]{1,0:T(8,128)(2,1)}, u32[]{:S(2)}, u32[]{:S(2)}) %collective-permute-start.3) | collective-permute-done | bytes 819232 | tf_op jit(solution)/shard_map/ppermute | solution.py:90
  119.5 0.0 copy-done.2
  119.5 3.5 %fusion.1 = f32[640,640]{1,0:T(8,128)S(1)} fusion(bf16[640,640]{1,0:T(8,128)(2,1)S(1)} %copy-done.2, f32[640,640]{1,0:T(8,128)} %fusion.6, bf16[1,1,640,640]{3,2,1,0:T(8,128)(2,1)S(1)} %copy-done, f32[]{:T(128)S(6)} %select_n.13, pred[640]{0:T(1024)(128)(4,1)S(1)} %iota_compare_fusion, bf16[640,640]{1,0:T(8,128)(2,1)} %get-tuple-element.8, ...), kind=kOutput, calls=%fused_computation.3 | convolution fusion | flops 1051852800 | bytes 6554244 | tf_op jit(solution)/shard_map/dot_general | solution.py:18
  123.0 71.0 %all-reduce.4 = bf16[640,640]{1,0:T(8,128)(2,1)} all-reduce(f32[640,640]{1,0:T(8,128)S(1)} %fusion.1), channel_id=1, replica_groups=mesh['sector'=32,'term'=16] {'term'}, use_global_device_ids=true, to_apply=%region_2.3 | all-reduce | flops 409600 | bytes 2457600 | tf_op jit(solution)/shard_map/psum | solution.py:102
  (1 shorter events, 0.0 us)
Async XLA Ops:
  0.0 18.0 %copy-start = (bf16[1,1,640,640]{3,2,1,0:T(8,128)(2,1)S(1)}, bf16[1,1,640,640]{3,2,1,0:T(8,128)(2,1)}, u32[]{:S(2)}) copy-start(bf16[1,1,640,640]{3,2,1,0:T(8,128)(2,1)} %param.7) | copy-start | bytes 2457604
  0.0 11.7 %copy-start.1 = (bf16[640,640]{1,0:T(8,128)(2,1)S(1)}, bf16[640,640]{1,0:T(8,128)(2,1)}, u32[]{:S(2)}) copy-start(bf16[640,640]{1,0:T(8,128)(2,1)} %param.5) | copy-start | bytes 2457604
  0.0 10.8 %collective-permute-start = (bf16[640,640]{1,0:T(8,128)(2,1)}, bf16[640,640]{1,0:T(8,128)(2,1)S(1)}, u32[]{:S(2)}, u32[]{:S(2)}) collective-permute-start(bf16[640,640]{1,0:T(8,128)(2,1)} %param.5), channel_id=1, source_target_pairs={{0,16},{16,0},{32,48},{48,32},{64,80},{80,64},{96,112},{112,96},{1... | collective-permute-start | bytes 2457608 | tf_op jit(solution)/shard_map/ppermute | solution.py:91
  2.1 16.0 %collective-permute-start.1 = (bf16[640,640]{1,0:T(8,128)(2,1)}, bf16[640,640]{1,0:T(8,128)(2,1)S(1)}, u32[]{:S(2)}, u32[]{:S(2)}) collective-permute-start(bf16[640,640]{1,0:T(8,128)(2,1)} %param.5), channel_id=1, source_target_pairs={{16,32},{48,64},{80,96},{112,128},{144,160},{176,192},{208,224},{2... | collective-permute-start | bytes 2457608 | tf_op jit(solution)/shard_map/ppermute | solution.py:90
  10.8 0.9 copy-start.4
  11.7 6.3 %copy-start.3 = (bf16[640,640]{1,0:T(8,128)(2,1)S(1)}, bf16[640,640]{1,0:T(8,128)(2,1)}, u32[]{:S(2)}) copy-start(bf16[640,640]{1,0:T(8,128)(2,1)} %get-tuple-element.8) | copy-start | bytes 2457604
  101.7 5.1 %collective-permute-start.2 = (bf16[640,640]{1,0:T(8,128)(2,1)S(1)}, bf16[640,640]{1,0:T(8,128)(2,1)}, u32[]{:S(2)}, u32[]{:S(2)}) collective-permute-start(bf16[640,640]{1,0:T(8,128)(2,1)S(1)} %pad_maximum_fusion), channel_id=1, source_target_pairs={{0,16},{16,0},{32,48},{48,32},{64,80},{80,64},{96,112},{112,96},{1... | collective-permute-start | bytes 2457608 | tf_op jit(solution)/shard_map/ppermute | solution.py:91
  103.6 15.9 %collective-permute-start.3 = (bf16[640,640]{1,0:T(8,128)(2,1)S(1)}, bf16[640,640]{1,0:T(8,128)(2,1)}, u32[]{:S(2)}, u32[]{:S(2)}) collective-permute-start(bf16[640,640]{1,0:T(8,128)(2,1)S(1)} %pad_maximum_fusion), channel_id=1, source_target_pairs={{16,32},{48,64},{80,96},{112,128},{144,160},{176,192},{208,224},{2... | collective-permute-start | bytes 2457608 | tf_op jit(solution)/shard_map/ppermute | solution.py:90
  106.7 12.8 %copy-start.2 = (bf16[640,640]{1,0:T(8,128)(2,1)S(1)}, bf16[640,640]{1,0:T(8,128)(2,1)}, u32[]{:S(2)}) copy-start(bf16[640,640]{1,0:T(8,128)(2,1)} %param.5) | copy-start | bytes 2457604
